TPU v7x, 256 devices: a 4x2x16 block of a 4x16x16 slice. The times are simulated.
256 devices in a mesh: group: 2 (over y), station: 16 (over z), tm: 4 (over x), chan: 2 (over core).
Axes of the slice: x: 4, y: 2, z: 16, core: 2. Of those that a mesh axis runs over, the one named last changes fastest.
The devices are a block of a 4x16x16 slice.
Arguments:
- voltages: bfloat16 [32, 128, 2, 96, 512], P(('group', 'station'), 'chan', None, None, 'tm'), parts along dimension 0, may hold values from -6 to 6
- delays: int32 [32], P(('group', 'station')), parts along dimension 0, may hold values from 0 to 16, as said below
- tap_sets: int32 [32, 128], P(('group', 'station'), 'chan'), parts along dimension 0, may hold values from 0 to 15
- tap_table: bfloat16 [16, 16], replicated, may hold values from -1.5 to 1.5
- weights: bfloat16 [32, 128, 2, 96, 128], P(('group', 'station'), 'chan'), parts along dimension 0, may hold values from -0.15625 to 0.15625
Outputs:
- array_beams: bfloat16 [256, 2, 128, 512], P(('group', 'chan', 'station'), None, None, 'tm'), parts along dimension 0
There are 2 independent parts, one for each index of `group`. A program takes and returns all parts, laid end to end along the dimension named above; an argument that names none is the same for every part. Nothing has to cross between parts.
Inputs may be any that keep to these rules, and one draw needn't show every extreme that they name: `delays`: every delay lies in 0 to 16, and some station has delay 16.
All inputs are finite; a program needn't handle non-finite values.
Results may differ from a plain program's by a relative error of at most 0.0049.
Values may be sent and summed in bfloat16 or wider, within the bound.
A program may use at most 64 MiB of HBM per device.

v0:
```python
import jax
import jax.numpy as jnp
from jax import lax
from jax.sharding import PartitionSpec as P

TAPS = 16
MAXD = 16
BLOCK = 128


def passed_along(value, axis, steps):
    count = lax.axis_size(axis)
    leading, last = (max(0, -steps), min(count, count - steps))
    return lax.ppermute(value, axis, [(source, source + steps) for source in range(leading, last)])


def steering_matrix(weights):
    real_w = weights[:, :, 0]
    imag_w = weights[:, :, 1]
    upper_rows = jnp.concatenate([real_w, imag_w], axis=-1)
    lower_rows = jnp.concatenate([-imag_w, real_w], axis=-1)
    return jnp.concatenate([upper_rows, lower_rows], axis=2)


def body(voltages, delays, tap_sets, tap_table, weights):
    station_number, channel_total, pairing_total, antenna_total, time_length = voltages.shape
    set_count, tap_count = tap_table.shape
    halo_len = MAXD + TAPS - 1
    window_len = BLOCK + halo_len
    flat_voltages = voltages.reshape(
        station_number, channel_total, pairing_total * antenna_total, time_length
    )
    prev_rim = passed_along(flat_voltages[..., time_length - halo_len :], "tm", 1)
    extended = jnp.concatenate([prev_rim, flat_voltages], axis=-1)
    windows = jnp.stack([extended], axis=3)
    set_onehot = (tap_sets[..., None] == jnp.arange(set_count)[None, None, :]).astype(jnp.bfloat16)
    chosen_taps = jnp.einsum(
        "scm,mk->sck", set_onehot, tap_table, preferred_element_type=jnp.float32
    ).astype(jnp.bfloat16)
    window_pos = jnp.arange(window_len)[:, None]
    output_pos = jnp.arange(BLOCK)[None, :]
    lag_table = output_pos + halo_len - window_pos
    station_lag = lag_table[None, :, :] - delays[:, None, None]
    tap_onehot = (station_lag[..., None] == jnp.arange(tap_count)[None, None, None, :]).astype(
        jnp.bfloat16
    )
    band_matrix = jnp.einsum(
        "sck,sjuk->scju", chosen_taps, tap_onehot, preferred_element_type=jnp.float32
    ).astype(jnp.bfloat16)
    delayed_voltages = jnp.einsum(
        "scanj,scju->scanu", windows, band_matrix, preferred_element_type=jnp.float32
    ).astype(jnp.bfloat16)
    delayed_voltages = delayed_voltages.reshape(
        station_number, channel_total, pairing_total * antenna_total, time_length
    )
    station_axis_size = lax.axis_size("station")
    row_count = channel_total // station_axis_size
    stacked = steering_matrix(weights)
    summed = lax.psum_scatter(
        jnp.einsum("scan,scat->cnt", stacked, delayed_voltages, preferred_element_type=jnp.float32),
        "station",
        scatter_dimension=0,
        tiled=True,
    )
    beam_count = weights.shape[-1]
    return summed.astype(jnp.bfloat16).reshape(row_count, 2, beam_count, time_length)


def solution(mesh):
    return jax.shard_map(
        body,
        mesh=mesh,
        in_specs=(
            P(("group", "station"), "chan", None, None, "tm"),
            P(("group", "station")),
            P(("group", "station"), "chan"),
            P(),
            P(("group", "station"), "chan", None, None, None),
        ),
        out_specs=P(("group", "chan", "station"), None, None, "tm"),
        check_vma=False,
    )
```

profile of v0, /device:TPU:44, one launch (start us, length us, event | category | flops | bytes accessed | tf_op | source)
XLA Modules:
  0.0 185.6 jit_solution(5500585693136973122)
XLA Ops:
  6.5 0.0 copy-start
  6.6 0.0 reduce-scatter.2.cloned.1.call-start
  6.6 4.5 %slice.12 = bf16[1,64,192,31]{3,2,1,0:T(8,128)(2,1)} slice(bf16[1,64,192,128]{3,2,1,0:T(8,128)(2,1)} %bitcast.30), slice={[0:1], [0:64], [0:192], [97:128]} | slice | bytes 1523712 | tf_op jit(solution)/shard_map/slice | solution.py:33
  11.0 0.0 copy-start.4
  11.1 0.0 copy-start.1
  11.1 4.6 %copy.13 = bf16[1,64,192,31]{2,1,3,0:T(8,128)(2,1)} copy(bf16[1,64,192,31]{3,2,1,0:T(8,128)(2,1)} %slice.12) | data formatting | bytes 1523712 | tf_op jit(solution)/shard_map/slice | solution.py:33
  15.7 3.3 %collective-permute-start = (bf16[1,64,192,31]{2,1,3,0:T(8,128)(2,1)}, bf16[1,64,192,31]{2,1,3,0:T(8,128)(2,1)}, u32[]{:S(2)}, u32[]{:S(2)}) collective-permute-start(bf16[1,64,192,31]{2,1,3,0:T(8,128)(2,1)} %copy.13), channel_id=1, source_target_pairs={{0,2},{2,4},{4,6},{1,3},{3,5},{5,7},{8,10},{10,12},{12,14},{9,11},... | collective-permute-start | bytes 2285576 | tf_op jit(solution)/shard_map/ppermute | solution.py:14
  19.6 0.0 copy-done
  19.7 0.0 copy-done.4
  19.7 2.6 %convolution_convert_fusion = bf16[64,159,128]{2,0,1:T(8,128)(2,1)} fusion(s32[159,128]{1,0:T(8,128)S(1)} %subtract_subtract_fusion, bf16[16,16]{1,0:T(8,128)(2,1)S(1)} %copy-done, s32[64]{0:T(128)S(1)} %bitcast.32), kind=kOutput, calls=%fused_computation.14 | convolution fusion | flops 43343872 | bytes 2687232 | tf_op jit(solution)/shard_map/sck,sjuk->scju/dot_general | solution.py:47
  22.3 0.0 copy-done.1
  22.3 5.0 %copy.15 = bf16[1,64,192,128]{2,3,1,0:T(8,128)(2,1)} copy(bf16[1,64,192,128]{3,2,1,0:T(8,128)(2,1)S(1)} %bitcast.31) | data formatting | bytes 6291456 | tf_op jit(solution)/shard_map/reshape | solution.py:30
  27.2 0.0 copy-start.2
  27.2 2.9 %fusion.22 = bf16[1,64,96,128]{3,2,1,0:T(8,128)(2,1)} fusion(bf16[1,64,2,96,128]{4,3,2,1,0:T(8,128)(2,1)} %param.9), kind=kLoop, calls=%fused_computation.26 | loop fusion | flops 786432 | bytes 3145728 | tf_op jit(solution)/shard_map/neg | solution.py:21
  30.1 0.0 copy-done.2
  30.1 0.0 copy-start.3
  30.1 1.8 slice_bitcast_fusion
  32.0 10.2 %collective-permute-done = bf16[1,64,192,31]{2,1,3,0:T(8,128)(2,1)} collective-permute-done((bf16[1,64,192,31]{2,1,3,0:T(8,128)(2,1)}, bf16[1,64,192,31]{2,1,3,0:T(8,128)(2,1)}, u32[]{:S(2)}, u32[]{:S(2)}) %collective-permute-start) | collective-permute-done | bytes 761888 | tf_op jit(solution)/shard_map/ppermute | solution.py:14
  42.2 2.8 %copy.14 = bf16[1,64,192,31]{2,3,1,0:T(8,128)(2,1)} copy(bf16[1,64,192,31]{2,1,3,0:T(8,128)(2,1)} %collective-permute-done) | data formatting | bytes 1523712 | tf_op jit(solution)/shard_map/ppermute | solution.py:14
  44.9 0.0 copy-done.3
  45.0 14.7 %fusion = f32[64,256,128]{2,1,0:T(8,128)} fusion(bf16[1,64,96,128]{3,2,1,0:T(8,128)(2,1)} %get-tuple-element.6, bf16[1,64,96,128]{3,2,1,0:T(8,128)(2,1)} %fusion.22, bf16[1,64,96,128]{3,2,1,0:T(8,128)(2,1)} %get-tuple-element.5, bf16[1,64,192,128]{2,3,1,0:T(8,128)(2,1)} %copy.15, bf16[1,64,192,31]{2,3,1,0:T(8,128)(2,1)} %copy.14, ...), kind=kOutput, calls=%fused_computation.1 | convolution fusion | flops 1340030976 | bytes 19619840 | tf_op jit(solution)/shard_map/scan,scat->cnt/dot_general | solution.py:60
  59.6 0.1 reduce-scatter.2.cloned.1.call-update
  59.7 117.3 %reduce-scatter.2.cloned.1.call-done = f32[4,256,128]{2,1,0:T(8,128)} async-done(((f32[64,256,128]{2,1,0:T(8,128)}), f32[4,256,128]{2,1,0:T(8,128)}) %reduce-scatter.2.cloned.1.call-update) | async-done | bytes 524304 | tf_op jit(solution)/shard_map/reduce_scatter | solution.py:59
  177.0 1.8 convert_element_type.20
  (2 shorter events, 0.0 us)
Async XLA Ops:
  6.5 13.1 %copy-start = (bf16[16,16]{1,0:T(8,128)(2,1)S(1)}, bf16[16,16]{1,0:T(8,128)(2,1)}, u32[]{:S(2)}) copy-start(bf16[16,16]{1,0:T(8,128)(2,1)} %param.8) | copy-start | bytes 1540
  6.6 170.4 %reduce-scatter.2.cloned.1.call-start = ((), (), s32[]{:S(2)}) async-start(), calls=%async_computation.1 | async-start | bytes 8912896 | tf_op jit(solution)/shard_map/reduce_scatter | solution.py:59
  11.0 8.6 %copy-start.4 = (s32[1,64]{1,0:T(1,128)S(1)}, s32[1,64]{1,0:T(1,128)}, u32[]{:S(2)}) copy-start(s32[1,64]{1,0:T(1,128)} %param.7) | copy-start | bytes 772
  11.1 11.2 %copy-start.1 = (bf16[1,64,2,96,128]{4,3,2,1,0:T(8,128)(2,1)S(1)}, bf16[1,64,2,96,128]{4,3,2,1,0:T(8,128)(2,1)}, u32[]{:S(2)}) copy-start(bf16[1,64,2,96,128]{4,3,2,1,0:T(8,128)(2,1)} %param.5) | copy-start | bytes 9437188
  15.7 26.5 %collective-permute-start = (bf16[1,64,192,31]{2,1,3,0:T(8,128)(2,1)}, bf16[1,64,192,31]{2,1,3,0:T(8,128)(2,1)}, u32[]{:S(2)}, u32[]{:S(2)}) collective-permute-start(bf16[1,64,192,31]{2,1,3,0:T(8,128)(2,1)} %copy.13), channel_id=1, source_target_pairs={{0,2},{2,4},{4,6},{1,3},{3,5},{5,7},{8,10},{10,12},{12,14},{9,11},... | collective-permute-start | bytes 2285576 | tf_op jit(solution)/shard_map/ppermute | solution.py:14
  27.2 2.9 %copy-start.2 = (bf16[1,64,2,96,128]{4,3,2,1,0:T(8,128)(2,1)S(1)}, bf16[1,64,2,96,128]{4,3,2,1,0:T(8,128)(2,1)}, u32[]{:S(2)}) copy-start(bf16[1,64,2,96,128]{4,3,2,1,0:T(8,128)(2,1)} %param.9) | copy-start | bytes 9437188
  30.1 14.8 %copy-start.3 = (bf16[64,159,128]{2,0,1:T(8,128)(2,1)S(1)}, bf16[64,159,128]{2,0,1:T(8,128)(2,1)}, u32[]{:S(2)}) copy-start(bf16[64,159,128]{2,0,1:T(8,128)(2,1)} %convolution_convert_fusion) | copy-start | bytes 7815172
Sparse Core Ops, SparseCore 0:
  59.8 117.1 reduce-scatter.1
where the time goes:
time: 187 us; the launch traced here: 186 us
  waiting for transfers between devices  128 us (68%)
  local copies, waits for them, and re-layouts  18.7 us (10%)
  matrix products  17.3 us (9%)
  between operations  14.1 us (8%)
  other arithmetic  4.7 us (3%)
  starting transfers between devices  3.26 us (2%)
    reduce_scatter x1, waiting for transfers between devices, body(): lax.psum_scatter(jnp.einsum('scan,scat->cnt', stacked, delayed_voltages,...  117 us
    dot_general x1, matrix products, body(): jnp.einsum('scan,scat->cnt', stacked, delayed_voltages, preferred_element...  14.7 us
    ppermute x1, waiting for transfers between devices, passed_along(): lax.ppermute(value, axis, [(source, source + steps) for source in range(l...  10.2 us
    slice x2, local copies, waits for them, and re-layouts, body(): flat_voltages[..., time_length - halo_len:]  9.14 us
    reshape x1, local copies, waits for them, and re-layouts, body(): voltages.reshape(station_number, channel_total, pairing_total * antenna_t...  4.95 us
  transfers between devices with their start and end apart: 2, of which 2 were waited for; matrix products, arithmetic and copies ran while one was open for 7% of the time, Pallas kernels for 0%

commit v1 on v0

v1 whole, which is shorter than its diff:
```python
import functools

import jax
import jax.numpy as jnp
from jax import lax
from jax.experimental import pallas as pl
from jax.experimental.pallas import tpu as pltpu
from jax.sharding import PartitionSpec as P

TAPS = 16
MAXD = 16
RIM = 32
MESH = pl.DeviceIdType.MESH
F32 = jnp.float32
BF16 = jnp.bfloat16


def dot_nt(left, right):
    return lax.dot_general(left, right, (((1,), (1,)), ((), ())), preferred_element_type=F32)


def kernel(
    ring,
    blocks,
    volt,
    steer,
    sets_hbm,
    delays,
    taps_hbm,
    out,
    sets,
    taps,
    vbuf,
    wbuf,
    rim_out,
    rim_in,
    band,
    band_rim,
    top,
    own,
    send,
    recv,
    small_sem,
    load_sem,
    rim_send,
    rim_recv,
    ring_send,
    ring_recv,
):
    me = lax.axis_index("station")
    block = lax.axis_index("tm")
    middle = ring // 2
    per = vbuf.shape[1]
    time = vbuf.shape[3]
    rows = vbuf.shape[2]
    antennas = rows // 2
    set_count = taps.shape[0]
    sides = (lax.rem(me + 1, ring), lax.rem(me + ring - 1, ring))

    barrier = pltpu.get_barrier_semaphore()
    for side in sides:
        pl.semaphore_signal(barrier, inc=1, device_id={"station": side}, device_id_type=MESH)

    @pl.when(block > 0)
    def _():
        pl.semaphore_signal(barrier, inc=1, device_id={"tm": block - 1}, device_id_type=MESH)

    @pl.when(block < blocks - 1)
    def _():
        pl.semaphore_signal(barrier, inc=1, device_id={"tm": block + 1}, device_id_type=MESH)

    def block_of(slot):
        odd = slot % 2
        distance = jnp.where(odd == 1, ring - (slot + 1) // 2, slot // 2)
        return lax.rem(me + middle + distance, ring)

    def load(slot, which):
        source, target = ((volt, vbuf), (steer, wbuf))[which]
        at = block_of(slot) * per
        return pltpu.make_async_copy(source.at[pl.ds(at, per)], target.at[slot], load_sem.at[slot, which])

    def start_loads(slot):
        load(slot, 0).start()
        load(slot, 1).start()

    small = [
        pltpu.make_async_copy(source, target, small_sem.at[index])
        for index, (source, target) in enumerate(((taps_hbm, taps), (sets_hbm, sets)))
    ]
    for copy in small:
        copy.start()
    for slot in range(3):
        start_loads(slot)
    for copy in small:
        copy.wait()

    delay = delays[0]
    table = taps[...].astype(F32)
    lane = lax.broadcasted_iota(jnp.int32, (set_count, time), 1)
    base = jnp.zeros((set_count, time), F32)
    for tap in range(TAPS):
        base = jnp.where((lane + (tap + delay)) % time == 0, table[:, tap : tap + 1], base)
    row_at = lax.broadcasted_iota(jnp.int32, (time, time), 0)
    col_at = lax.broadcasted_iota(jnp.int32, (time, time), 1)
    for index in range(set_count):
        spread = jnp.broadcast_to(base[index : index + 1], (time, time))
        turned = pltpu.roll(spread, 0, 1, stride=1, stride_axis=0)
        band[index] = jnp.where(col_at <= row_at, turned, 0.0).astype(BF16)
        turned = pltpu.roll(spread[:RIM], RIM, 1, stride=1, stride_axis=0)
        band_rim[index] = turned[:, :RIM].astype(BF16)

    pick_row = lax.broadcasted_iota(jnp.int32, (RIM, time), 0)
    pick_col = lax.broadcasted_iota(jnp.int32, (RIM, time), 1)
    pick = jnp.where(pick_col == pick_row + (time - RIM), 1.0, 0.0).astype(BF16)

    def rim_copy(slot):
        return pltpu.make_async_remote_copy(
            src_ref=rim_out.at[slot],
            dst_ref=rim_in.at[slot],
            send_sem=rim_send.at[slot],
            recv_sem=rim_recv.at[slot],
            device_id={"tm": lax.rem(block + 1, blocks)},
            device_id_type=MESH,
        )

    def send_rim(slot):
        @pl.when(block < blocks - 1)
        def _():
            for ch in range(per):
                rim_out[slot, ch] = dot_nt(pick, vbuf[slot, ch]).astype(BF16)
            rim_copy(slot).start()

    def wait_rim(slot):
        @pl.when(block > 0)
        def _():
            rim_copy(slot).wait_recv()

    @pl.when(block == 0)
    def _():
        rim_in[...] = jnp.zeros_like(rim_in)

    def steering(slot, ch):
        real_w = wbuf[slot, ch, :antennas]
        imag_w = wbuf[slot, ch, antennas:]
        upper = jnp.concatenate([real_w, imag_w], axis=1)
        lower = jnp.concatenate([-imag_w, real_w], axis=1)
        return jnp.concatenate([upper, lower], axis=0)

    def filtered(slot, ch):
        chosen = sets[0, block_of(slot) * per + ch]
        return chosen, dot_nt(band[chosen], vbuf[slot, ch])

    def with_rim(slot, ch, chosen, early):
        return early + jnp.dot(band_rim[chosen], rim_in[slot, ch], preferred_element_type=F32)

    def beams(slot, ch):
        chosen, full = filtered(slot, ch)
        early = with_rim(slot, ch, chosen, full[:RIM])
        delayed = jnp.concatenate([early, full[RIM:]], axis=0).astype(BF16)
        return jnp.dot(delayed, steering(slot, ch), preferred_element_type=F32)

    def ring_copy(way, step, ch, part=None):
        span = pl.ds(0, time) if part is None else part
        return pltpu.make_async_remote_copy(
            src_ref=send.at[way, step, ch, span],
            dst_ref=recv.at[way, step, ch, span],
            send_sem=ring_send.at[way, step, ch],
            recv_sem=ring_recv.at[way, step, ch],
            device_id={"station": sides[way]},
            device_id_type=MESH,
        )

    half = per // 2
    order = ([(q + half) % per for q in range(per)], list(range(per)))
    first_way = [0 if ch < half else 1 for ch in range(per)]

    load(0, 0).wait()
    greeters = 2 + jnp.where(block > 0, 1, 0) + jnp.where(block < blocks - 1, 1, 0)
    pl.semaphore_wait(barrier, greeters)
    send_rim(0)
    for slot in range(3, ring):
        start_loads(slot)
    load(0, 1).wait()
    early_span, late_span = pl.ds(0, RIM), pl.ds(RIM, time - RIM)
    for q in range(half):
        for ch in (q, q + half):
            way = first_way[ch]
            chosen, full = filtered(0, ch)
            top[ch] = full[:RIM]
            late = jnp.dot(full[RIM:].astype(BF16), steering(0, ch), preferred_element_type=F32)
            send[way, 0, ch, RIM:] = late.astype(BF16)
            ring_copy(way, 0, ch, late_span).start()
    for slot in (1, 2):
        load(slot, 0).wait()
        send_rim(slot)
    wait_rim(0)
    for q in range(half):
        for ch in (q, q + half):
            way = first_way[ch]
            early = with_rim(0, ch, sets[0, block_of(0) * per + ch], top[ch]).astype(BF16)
            early = jnp.dot(early, steering(0, ch), preferred_element_type=F32)
            send[way, 0, ch, :RIM] = early.astype(BF16)
            ring_copy(way, 0, ch, early_span).start()
    for slot in (1, 2):
        load(slot, 1).wait()
        wait_rim(slot)
    for q in range(per):
        for way in (0, 1):
            own[1, way, order[way][q]] = beams(1 + way, order[way][q])
    for slot in (3, 4):
        if slot < ring:
            load(slot, 0).wait()
            send_rim(slot)

    def one_step(step, first, last):
        now, later = step % 2, (step + 1) % 2
        coming = (2 * step + 1,) if last else (2 * step + 1, 2 * step + 2)
        for q in range(per):
            for way in (0, 1):
                ch = order[way][q]
                total = own[now, way, ch]
                if not first or q >= half:
                    ring_copy(way, step - 1, ch).wait_recv()
                    total = total + recv[way, step - 1, ch].astype(F32)
                send[way, step, ch] = total.astype(BF16)
                ring_copy(way, step, ch).start()
            if q == 0:
                for slot in coming:
                    load(slot, 1).wait()
                    wait_rim(slot)
            for way, slot in enumerate(coming):
                ch = order[way][q]
                own[later, way, ch] = beams(slot, ch)

    def prepare(slots):
        for slot in slots:
            load(slot, 0).wait()
            send_rim(slot)

    for step in range(1, middle):
        if 2 <= step < middle - 2:
            continue
        if step == middle - 2 and middle - 2 > 2:

            @pl.loop(2, middle - 2)
            def _(at):
                one_step(at, False, False)
                prepare((2 * at + 3, 2 * at + 4))

        one_step(step, step == 1, step == middle - 1)
        if step + 2 < middle:
            prepare((2 * step + 3, 2 * step + 4))
        elif step + 2 == middle:
            prepare((2 * step + 3,))

    end = middle % 2
    for q in range(per):
        for way in (0, 1):
            ch = order[way][q]
            ring_copy(way, middle - 1, ch).wait_recv()
            total = own[end, 0, ch] + recv[way, middle - 1, ch].astype(F32)
            if q < half:
                own[end, 0, ch] = total
            else:
                out[ch] = total.T.astype(BF16)

    for ch in range(per):
        ring_copy(first_way[ch], 0, ch).wait_send()

    @pl.loop(1, middle)
    def _(at):
        for way in (0, 1):
            for ch in range(per):
                ring_copy(way, at, ch).wait_send()

    @pl.when(block < blocks - 1)
    def _():
        @pl.loop(0, ring)
        def _(slot):
            rim_copy(slot).wait_send()


def body(ring, blocks, voltages, delays, tap_sets, tap_table, weights):
    _, channels, parts, antennas, time = voltages.shape
    beams = weights.shape[-1]
    per = channels // ring
    rows = parts * antennas
    middle = ring // 2
    set_count = tap_table.shape[0]
    out = pl.pallas_call(
        functools.partial(kernel, ring, blocks),
        out_shape=jax.ShapeDtypeStruct((per, 2 * beams, time), BF16),
        in_specs=[
            pl.BlockSpec(memory_space=pltpu.HBM),
            pl.BlockSpec(memory_space=pltpu.HBM),
            pl.BlockSpec(memory_space=pltpu.HBM),
            pl.BlockSpec(memory_space=pltpu.SMEM),
            pl.BlockSpec(memory_space=pltpu.HBM),
        ],
        out_specs=pl.BlockSpec(memory_space=pltpu.VMEM),
        scratch_shapes=[
            pltpu.SMEM(tap_sets.shape, jnp.int32),
            pltpu.VMEM(tap_table.shape, BF16),
            pltpu.VMEM((ring, per, rows, time), BF16),
            pltpu.VMEM((ring, per, rows, beams), BF16),
            pltpu.VMEM((ring, per, RIM, rows), BF16),
            pltpu.VMEM((ring, per, RIM, rows), BF16),
            pltpu.VMEM((set_count, time, time), BF16),
            pltpu.VMEM((set_count, RIM, RIM), BF16),
            pltpu.VMEM((per, RIM, rows), F32),
            pltpu.VMEM((2, 2, per, time, 2 * beams), F32),
            pltpu.VMEM((2, middle, per, time, 2 * beams), BF16),
            pltpu.VMEM((2, middle, per, time, 2 * beams), BF16),
            pltpu.SemaphoreType.DMA((2,)),
            pltpu.SemaphoreType.DMA((ring, 2)),
            pltpu.SemaphoreType.DMA((ring,)),
            pltpu.SemaphoreType.DMA((ring,)),
            pltpu.SemaphoreType.DMA((2, middle, per)),
            pltpu.SemaphoreType.DMA((2, middle, per)),
        ],
        compiler_params=pltpu.CompilerParams(
            collective_id=0, has_side_effects=True, vmem_limit_bytes=63 * 1024 * 1024
        ),
    )(
        voltages.reshape(channels, rows, time),
        weights.reshape(channels, rows, beams),
        tap_sets,
        delays,
        tap_table,
    )
    return out.reshape(per, 2, beams, time)


def solution(mesh):
    return jax.shard_map(
        functools.partial(body, mesh.shape["station"], mesh.shape["tm"]),
        mesh=mesh,
        in_specs=(
            P(("group", "station"), "chan", None, None, "tm"),
            P(("group", "station")),
            P(("group", "station"), "chan"),
            P(),
            P(("group", "station"), "chan", None, None, None),
        ),
        out_specs=P(("group", "chan", "station"), None, None, "tm"),
        check_vma=False,
    )
```

time: 187 us -> 79.5 us (0.43)
  waiting for transfers between devices: 128 us -> 0 us
  Pallas kernels: 0 us -> 76 us
  matrix products: 17.3 us -> 0 us
  local copies, waits for them, and re-layouts: 18.7 us -> 1.67 us
  between operations: 14.1 us -> 0.66 us
  other arithmetic: 4.7 us -> 0 us
  starting transfers between devices: 3.26 us -> 0 us
    reduce_scatter x1 -> x0, waiting for transfers between devices: 117 us -> none  [body(): lax.psum_scatter(jnp.einsum('scan,scat->cnt', stacked, delayed_voltages,...]
    pallas_call x0 -> x1, Pallas kernels: none -> 76 us  [body(): pl.pallas_call(functools.partial(kernel, ring, blocks), out_shape=jax.Sha...]
    dot_general x2 -> x0, matrix products: 17.3 us -> none  [the longest x1 14.7 us: body(): jnp.einsum('scan,scat->cnt', stacked, delayed_voltages, preferred_element...]
    ppermute x1 -> x0, waiting for transfers between devices: 10.2 us -> none  [passed_along(): lax.ppermute(value, axis, [(source, source + steps) for source in range(l...]
    slice x2 -> x0, local copies, waits for them, and re-layouts: 9.14 us -> none  [body(): flat_voltages[..., time_length - halo_len:]]
    reshape x1 -> x0, local copies, waits for them, and re-layouts: 4.95 us -> none  [body(): voltages.reshape(station_number, channel_total, pairing_total * antenna_t...]
    ppermute x1 -> x0, starting transfers between devices: 3.26 us -> none  [passed_along(): lax.ppermute(value, axis, [(source, source + steps) for source in range(l...]
    neg x1 -> x0, other arithmetic: 2.9 us -> none  [steering_matrix(): lower_rows = jnp.concatenate([-imag_w, real_w], axis=-1)]
  transfers between devices with their start and end apart: 2 -> 0, of which waited for: 2 -> 0; matrix products, arithmetic and copies ran while one was open for 7% -> 0% of each run, Pallas kernels for 0% -> 0%
where the time goes in v1:
time: 79.5 us; the launch traced here: 78.3 us
  Pallas kernels  76 us (96%)
  local copies, waits for them, and re-layouts  1.67 us (2%)
    pallas_call x1, Pallas kernels, body(): pl.pallas_call(functools.partial(kernel, ring, blocks), out_shape=jax.Sha...  76 us
    unnamed x1, local copies, waits for them, and re-layouts  1.67 us

profile of v1, /device:TPU:44, one launch (start us, length us, event | category | flops | bytes accessed | tf_op | source)
XLA Modules:
  0.0 78.3 jit_solution(15307327186436634908)
XLA Ops:
  0.7 76.0 %shard_map.55 = bf16[4,256,128]{2,1,0:T(8,128)(2,1)} custom-call(bf16[64,192,128]{2,1,0:T(8,128)(2,1)} %bitcast.3, bf16[64,192,128]{2,1,0:T(8,128)(2,1)} %bitcast.4, s32[1,64]{1,0:T(1,128)} %sets_hbm.1, s32[1]{0:T(128)S(6)} %copy.7.delays, bf16[16,16]{1,0:T(8,128)(2,1)} %taps_hbm.1), custom_call_target="tpu_custom_call" | custom-call | tf_op jit(solution)/shard_map/pallas_call | solution.py:290
  76.6 1.7 %copy.8 = bf16[4,2,128,128]{3,2,1,0:T(8,128)(2,1)} copy(bf16[4,2,128,128]{3,2,1,0:T(8,128)(2,1)} %bitcast.5) | data formatting | bytes 524288

commit v2 on v1

--- a/solution.py
+++ b/solution.py
@@ -13,6 +13,14 @@
 MESH = pl.DeviceIdType.MESH
 F32 = jnp.float32
 BF16 = jnp.bfloat16
+
+
+RIGHT, LEFT = 0, 1
+
+
+def lengths(ring):
+    right = max(2, (ring - 1) * 2 // 5)
+    return right, ring - 1 - right
 
 
 def dot_nt(left, right):
@@ -49,13 +57,13 @@
 ):
     me = lax.axis_index("station")
     block = lax.axis_index("tm")
-    middle = ring // 2
     per = vbuf.shape[1]
     time = vbuf.shape[3]
     rows = vbuf.shape[2]
     antennas = rows // 2
     set_count = taps.shape[0]
     sides = (lax.rem(me + 1, ring), lax.rem(me + ring - 1, ring))
+    right_len, left_len = lengths(ring)
 
     barrier = pltpu.get_barrier_semaphore()
     for side in sides:
@@ -69,10 +77,17 @@
     def _():
         pl.semaphore_signal(barrier, inc=1, device_id={"tm": block + 1}, device_id_type=MESH)
 
+    def left_slot(step):
+        return jnp.where(step < right_len, 2 * step, step + right_len)
+
+    def right_slot(step):
+        return 2 * step + 1
+
     def block_of(slot):
-        odd = slot % 2
-        distance = jnp.where(odd == 1, ring - (slot + 1) // 2, slot // 2)
-        return lax.rem(me + middle + distance, ring)
+        ahead = right_len - slot // 2
+        behind = left_len - slot // 2
+        paired = jnp.where(slot % 2 == 1, ahead, ring - behind)
+        return lax.rem(me + jnp.where(slot < 2 * right_len, paired, slot + 1), ring)
 
     def load(slot, which):
         source, target = ((volt, vbuf), (steer, wbuf))[which]
@@ -89,7 +104,7 @@
     ]
     for copy in small:
         copy.start()
-    for slot in range(3):
+    for slot in range(4):
         start_loads(slot)
     for copy in small:
         copy.wait()
@@ -159,119 +174,117 @@
         delayed = jnp.concatenate([early, full[RIM:]], axis=0).astype(BF16)
         return jnp.dot(delayed, steering(slot, ch), preferred_element_type=F32)
 
-    def ring_copy(way, step, ch, part=None):
+    def ring_copy(way, slot, ch, part=None):
         span = pl.ds(0, time) if part is None else part
         return pltpu.make_async_remote_copy(
-            src_ref=send.at[way, step, ch, span],
-            dst_ref=recv.at[way, step, ch, span],
-            send_sem=ring_send.at[way, step, ch],
-            recv_sem=ring_recv.at[way, step, ch],
+            src_ref=send.at[slot, ch, span],
+            dst_ref=recv.at[slot, ch, span],
+            send_sem=ring_send.at[slot, ch],
+            recv_sem=ring_recv.at[slot, ch],
             device_id={"station": sides[way]},
             device_id_type=MESH,
         )
 
-    half = per // 2
-    order = ([(q + half) % per for q in range(per)], list(range(per)))
-    first_way = [0 if ch < half else 1 for ch in range(per)]
-
-    load(0, 0).wait()
+    def prepare(slot):
+        load(slot, 0).wait()
+        send_rim(slot)
+
+    firsts = ((LEFT, 0), (RIGHT, 1))
+    for _, slot in firsts:
+        load(slot, 0).wait()
     greeters = 2 + jnp.where(block > 0, 1, 0) + jnp.where(block < blocks - 1, 1, 0)
     pl.semaphore_wait(barrier, greeters)
-    send_rim(0)
-    for slot in range(3, ring):
+    for _, slot in firsts:
+        send_rim(slot)
+    for slot in range(4, ring):
         start_loads(slot)
-    load(0, 1).wait()
+    for _, slot in firsts:
+        load(slot, 1).wait()
     early_span, late_span = pl.ds(0, RIM), pl.ds(RIM, time - RIM)
-    for q in range(half):
-        for ch in (q, q + half):
-            way = first_way[ch]
-            chosen, full = filtered(0, ch)
-            top[ch] = full[:RIM]
-            late = jnp.dot(full[RIM:].astype(BF16), steering(0, ch), preferred_element_type=F32)
-            send[way, 0, ch, RIM:] = late.astype(BF16)
-            ring_copy(way, 0, ch, late_span).start()
-    for slot in (1, 2):
-        load(slot, 0).wait()
-        send_rim(slot)
-    wait_rim(0)
-    for q in range(half):
-        for ch in (q, q + half):
-            way = first_way[ch]
-            early = with_rim(0, ch, sets[0, block_of(0) * per + ch], top[ch]).astype(BF16)
-            early = jnp.dot(early, steering(0, ch), preferred_element_type=F32)
-            send[way, 0, ch, :RIM] = early.astype(BF16)
-            ring_copy(way, 0, ch, early_span).start()
-    for slot in (1, 2):
+    for ch in range(per):
+        for way, slot in firsts:
+            chosen, full = filtered(slot, ch)
+            top[slot, ch] = full[:RIM]
+            late = jnp.dot(full[RIM:].astype(BF16), steering(slot, ch), preferred_element_type=F32)
+            send[slot, ch, RIM:] = late.astype(BF16)
+            ring_copy(way, slot, ch, late_span).start()
+    for slot in (2, 3):
+        prepare(slot)
+    for _, slot in firsts:
+        wait_rim(slot)
+    for ch in range(per):
+        for way, slot in firsts:
+            early = with_rim(slot, ch, sets[0, block_of(slot) * per + ch], top[slot, ch]).astype(BF16)
+            early = jnp.dot(early, steering(slot, ch), preferred_element_type=F32)
+            send[slot, ch, :RIM] = early.astype(BF16)
+            ring_copy(way, slot, ch, early_span).start()
+    for slot in (4, 5):
+        prepare(slot)
+    for slot in (2, 3):
         load(slot, 1).wait()
         wait_rim(slot)
-    for q in range(per):
-        for way in (0, 1):
-            own[1, way, order[way][q]] = beams(1 + way, order[way][q])
-    for slot in (3, 4):
-        if slot < ring:
-            load(slot, 0).wait()
-            send_rim(slot)
-
-    def one_step(step, first, last):
-        now, later = step % 2, (step + 1) % 2
-        coming = (2 * step + 1,) if last else (2 * step + 1, 2 * step + 2)
-        for q in range(per):
-            for way in (0, 1):
-                ch = order[way][q]
-                total = own[now, way, ch]
-                if not first or q >= half:
-                    ring_copy(way, step - 1, ch).wait_recv()
-                    total = total + recv[way, step - 1, ch].astype(F32)
-                send[way, step, ch] = total.astype(BF16)
-                ring_copy(way, step, ch).start()
-            if q == 0:
-                for slot in coming:
-                    load(slot, 1).wait()
-                    wait_rim(slot)
-            for way, slot in enumerate(coming):
-                ch = order[way][q]
-                own[later, way, ch] = beams(slot, ch)
-
-    def prepare(slots):
-        for slot in slots:
-            load(slot, 0).wait()
-            send_rim(slot)
-
-    for step in range(1, middle):
-        if 2 <= step < middle - 2:
-            continue
-        if step == middle - 2 and middle - 2 > 2:
-
-            @pl.loop(2, middle - 2)
-            def _(at):
-                one_step(at, False, False)
-                prepare((2 * at + 3, 2 * at + 4))
-
-        one_step(step, step == 1, step == middle - 1)
-        if step + 2 < middle:
-            prepare((2 * step + 3, 2 * step + 4))
-        elif step + 2 == middle:
-            prepare((2 * step + 3,))
-
-    end = middle % 2
-    for q in range(per):
-        for way in (0, 1):
-            ch = order[way][q]
-            ring_copy(way, middle - 1, ch).wait_recv()
-            total = own[end, 0, ch] + recv[way, middle - 1, ch].astype(F32)
-            if q < half:
-                own[end, 0, ch] = total
-            else:
-                out[ch] = total.T.astype(BF16)
-
     for ch in range(per):
-        ring_copy(first_way[ch], 0, ch).wait_send()
-
-    @pl.loop(1, middle)
-    def _(at):
-        for way in (0, 1):
-            for ch in range(per):
-                ring_copy(way, at, ch).wait_send()
+        for slot in (2, 3):
+            own[slot, ch] = beams(slot, ch)
+    for slot in (6, 7):
+        prepare(slot)
+
+    lag = jnp.clip((right_len + 2 - me) // 2, 0, left_len - right_len)
+
+    def pass_on(way, before, slot, ch):
+        ring_copy(way, before, ch).wait_recv()
+        total = own[slot, ch] + recv[before, ch].astype(F32)
+        send[slot, ch] = total.astype(BF16)
+        ring_copy(way, slot, ch).start()
+
+    @pl.loop(1, left_len)
+    def _(step):
+        other = step - lag
+        right_on = jnp.logical_and(other >= 1, other < right_len)
+        now, later = left_slot(step), left_slot(step + 1)
+        right_later = jnp.minimum(right_slot(step + 1), 2 * right_len - 1)
+        right_more = step + 1 < right_len
+        for ch in range(per):
+            pass_on(LEFT, left_slot(step - 1), now, ch)
+
+            @pl.when(right_on)
+            def _():
+                pass_on(RIGHT, right_slot(other - 1), right_slot(other), ch)
+
+            if ch == 0:
+                load(later, 1).wait()
+                wait_rim(later)
+
+                @pl.when(right_more)
+                def _():
+                    load(right_later, 1).wait()
+                    wait_rim(right_later)
+
+            own[later, ch] = beams(later, ch)
+
+            @pl.when(right_more)
+            def _():
+                own[right_later, ch] = beams(right_later, ch)
+
+        @pl.when(step + 3 <= left_len)
+        def _():
+            prepare(left_slot(step + 3))
+
+        @pl.when(step + 3 < right_len)
+        def _():
+            prepare(jnp.minimum(right_slot(step + 3), 2 * right_len - 1))
+
+    for ch in range(per):
+        total = own[ring - 1, ch]
+        for way, slot in ((RIGHT, 2 * right_len - 1), (LEFT, ring - 2)):
+            ring_copy(way, slot, ch).wait_recv()
+            total = total + recv[slot, ch].astype(F32)
+        out[ch] = total.T.astype(BF16)
+
+    @pl.loop(0, ring - 1)
+    def _(slot):
+        for ch in range(per):
+            ring_copy(LEFT, slot, ch).wait_send()
 
     @pl.when(block < blocks - 1)
     def _():
@@ -285,7 +298,6 @@
     beams = weights.shape[-1]
     per = channels // ring
     rows = parts * antennas
-    middle = ring // 2
     set_count = tap_table.shape[0]
     out = pl.pallas_call(
         functools.partial(kernel, ring, blocks),
@@ -307,16 +319,16 @@
             pltpu.VMEM((ring, per, RIM, rows), BF16),
             pltpu.VMEM((set_count, time, time), BF16),
             pltpu.VMEM((set_count, RIM, RIM), BF16),
-            pltpu.VMEM((per, RIM, rows), F32),
-            pltpu.VMEM((2, 2, per, time, 2 * beams), F32),
-            pltpu.VMEM((2, middle, per, time, 2 * beams), BF16),
-            pltpu.VMEM((2, middle, per, time, 2 * beams), BF16),
+            pltpu.VMEM((2, per, RIM, rows), F32),
+            pltpu.VMEM((ring, per, time, 2 * beams), F32),
+            pltpu.VMEM((ring - 1, per, time, 2 * beams), BF16),
+            pltpu.VMEM((ring - 1, per, time, 2 * beams), BF16),
             pltpu.SemaphoreType.DMA((2,)),
             pltpu.SemaphoreType.DMA((ring, 2)),
             pltpu.SemaphoreType.DMA((ring,)),
             pltpu.SemaphoreType.DMA((ring,)),
-            pltpu.SemaphoreType.DMA((2, middle, per)),
-            pltpu.SemaphoreType.DMA((2, middle, per)),
+            pltpu.SemaphoreType.DMA((ring - 1, per)),
+            pltpu.SemaphoreType.DMA((ring - 1, per)),
         ],
         compiler_params=pltpu.CompilerParams(
             collective_id=0, has_side_effects=True, vmem_limit_bytes=63 * 1024 * 1024

time: 79.5 us -> 81.9 us (1.030)
  Pallas kernels: 76 us -> 79 us
    pallas_call x1, Pallas kernels: 76 us -> 79 us  [body(): pl.pallas_call(functools.partial(kernel, ring, blocks), out_shape=jax.Sha...]
where the time goes in v2:
time: 81.9 us; the launch traced here: 81.3 us
  Pallas kernels  79 us (96%)
  local copies, waits for them, and re-layouts  1.67 us (2%)
    pallas_call x1, Pallas kernels, body(): pl.pallas_call(functools.partial(kernel, ring, blocks), out_shape=jax.Sha...  79 us
    unnamed x1, local copies, waits for them, and re-layouts  1.67 us

profile of v2, /device:TPU:44, one launch (start us, length us, event | category | flops | bytes accessed | tf_op | source)
XLA Modules:
  0.0 81.3 jit_solution(8635174471020880313)
XLA Ops:
  0.7 79.0 %shard_map.55 = bf16[4,256,128]{2,1,0:T(8,128)(2,1)} custom-call(bf16[64,192,128]{2,1,0:T(8,128)(2,1)} %bitcast.3, bf16[64,192,128]{2,1,0:T(8,128)(2,1)} %bitcast.4, s32[1,64]{1,0:T(1,128)} %sets_hbm.1, s32[1]{0:T(128)S(6)} %copy.7.delays, bf16[16,16]{1,0:T(8,128)(2,1)} %taps_hbm.1), custom_call_target="tpu_custom_call" | custom-call | tf_op jit(solution)/shard_map/pallas_call | solution.py:302
  79.7 1.7 %copy.8 = bf16[4,2,128,128]{3,2,1,0:T(8,128)(2,1)} copy(bf16[4,2,128,128]{3,2,1,0:T(8,128)(2,1)} %bitcast.5) | data formatting | bytes 524288

commit v3 on v1

--- a/solution.py
+++ b/solution.py
@@ -207,10 +207,9 @@
     for q in range(per):
         for way in (0, 1):
             own[1, way, order[way][q]] = beams(1 + way, order[way][q])
-    for slot in (3, 4):
-        if slot < ring:
-            load(slot, 0).wait()
-            send_rim(slot)
+    for slot in range(3, min(7, ring)):
+        load(slot, 0).wait()
+        send_rim(slot)
 
     def one_step(step, first, last):
         now, later = step % 2, (step + 1) % 2
@@ -232,10 +231,9 @@
                 ch = order[way][q]
                 own[later, way, ch] = beams(slot, ch)
 
-    def prepare(slots):
-        for slot in slots:
-            load(slot, 0).wait()
-            send_rim(slot)
+    def prepare(slot):
+        load(slot, 0).wait()
+        send_rim(slot)
 
     for step in range(1, middle):
         if 2 <= step < middle - 2:
@@ -245,13 +243,16 @@
             @pl.loop(2, middle - 2)
             def _(at):
                 one_step(at, False, False)
-                prepare((2 * at + 3, 2 * at + 4))
+                prepare(2 * at + 5)
+
+                @pl.when(2 * at + 6 < ring)
+                def _():
+                    prepare(jnp.minimum(2 * at + 6, ring - 1))
 
         one_step(step, step == 1, step == middle - 1)
-        if step + 2 < middle:
-            prepare((2 * step + 3, 2 * step + 4))
-        elif step + 2 == middle:
-            prepare((2 * step + 3,))
+        for slot in (2 * step + 5, 2 * step + 6):
+            if slot < ring:
+                prepare(slot)
 
     end = middle % 2
     for q in range(per):

time: 79.5 us -> 79.3 us (level); the launches traced: 78.3 us -> 79 us
  no operation moved by 1% of the time
where the time goes in v3:
time: 79.3 us; the launch traced here: 79 us
  Pallas kernels  76.7 us (97%)
  local copies, waits for them, and re-layouts  1.67 us (2%)
    pallas_call x1, Pallas kernels, body(): pl.pallas_call(functools.partial(kernel, ring, blocks), out_shape=jax.Sha...  76.7 us
    unnamed x1, local copies, waits for them, and re-layouts  1.67 us

profile of v3, /device:TPU:44, one launch (start us, length us, event | category | flops | bytes accessed | tf_op | source)
XLA Modules:
  0.0 79.0 jit_solution(10930685804602123190)
XLA Ops:
  0.7 76.7 %shard_map.55 = bf16[4,256,128]{2,1,0:T(8,128)(2,1)} custom-call(bf16[64,192,128]{2,1,0:T(8,128)(2,1)} %bitcast.3, bf16[64,192,128]{2,1,0:T(8,128)(2,1)} %bitcast.4, s32[1,64]{1,0:T(1,128)} %sets_hbm.1, s32[1]{0:T(128)S(6)} %copy.7.delays, bf16[16,16]{1,0:T(8,128)(2,1)} %taps_hbm.1), custom_call_target="tpu_custom_call" | custom-call | tf_op jit(solution)/shard_map/pallas_call | solution.py:291
  77.3 1.7 %copy.8 = bf16[4,2,128,128]{3,2,1,0:T(8,128)(2,1)} copy(bf16[4,2,128,128]{3,2,1,0:T(8,128)(2,1)} %bitcast.5) | data formatting | bytes 524288

commit v4 on v3

v4 whole, which is shorter than its diff:
```python
import functools

import jax
import jax.numpy as jnp
from jax import lax
from jax.experimental import pallas as pl
from jax.experimental.pallas import tpu as pltpu
from jax.sharding import PartitionSpec as P

TAPS = 16
MAXD = 16
RIM = 32
MESH = pl.DeviceIdType.MESH
F32 = jnp.float32
BF16 = jnp.bfloat16


RIGHT, LEFT = 0, 1
CUT = 2


def dot_nt(left, right):
    return lax.dot_general(left, right, (((1,), (1,)), ((), ())), preferred_element_type=F32)


def kernel(
    ring,
    blocks,
    volt,
    steer,
    sets_hbm,
    delays,
    taps_hbm,
    out,
    sets,
    taps,
    vbuf,
    wbuf,
    rim_out,
    rim_in,
    band,
    band_rim,
    top,
    own,
    send,
    recv,
    small_sem,
    load_sem,
    rim_send,
    rim_recv,
    behind_in,
    ring_send,
    ring_recv,
):
    me = lax.axis_index("station")
    block = lax.axis_index("tm")
    per = vbuf.shape[1]
    time = vbuf.shape[3]
    rows = vbuf.shape[2]
    antennas = rows // 2
    set_count = taps.shape[0]
    middle, half = ring // 2, per // 2
    sides = (lax.rem(me + 1, ring), lax.rem(me + ring - 1, ring))

    barrier = pltpu.get_barrier_semaphore()
    pl.semaphore_signal(barrier, inc=1, device_id={"station": sides[LEFT]}, device_id_type=MESH)

    @pl.when(block > 0)
    def _():
        pl.semaphore_signal(barrier, inc=1, device_id={"tm": block - 1}, device_id_type=MESH)

    def reach(way, target, ch):
        right = middle - ch // half
        inner = jnp.logical_and(target >= middle - CUT, target < middle + CUT)
        right = jnp.where(inner, target, right)
        return right if way == RIGHT else ring - 1 - right

    furthest = middle + max(CUT - 1, 0)

    def target_of(way, hops):
        return lax.rem(me + ring + (hops if way == RIGHT else -hops), ring)

    def slot_of(way, hops):
        nearer = middle - hops
        near = 2 * nearer - 1 if way == RIGHT else 2 * nearer
        far = -2 * nearer if way == RIGHT else -2 * nearer - 1
        if isinstance(hops, int):
            return near if nearer > 0 else max(far, 0)
        return jnp.where(nearer > 0, near, jnp.maximum(far, 0))

    def block_of(slot):
        odd = slot % 2
        distance = jnp.where(odd == 1, ring - (slot + 1) // 2, slot // 2)
        return lax.rem(me + middle + distance, ring)

    def load(slot, which):
        source, target = ((volt, vbuf), (steer, wbuf))[which]
        at = block_of(slot) * per
        return pltpu.make_async_copy(source.at[pl.ds(at, per)], target.at[slot], load_sem.at[slot, which])

    def start_loads(slot):
        load(slot, 0).start()
        load(slot, 1).start()

    small = [
        pltpu.make_async_copy(source, target, small_sem.at[index])
        for index, (source, target) in enumerate(((taps_hbm, taps), (sets_hbm, sets)))
    ]
    for copy in small:
        copy.start()
    for slot in range(3):
        start_loads(slot)
    for copy in small:
        copy.wait()

    delay = delays[0]
    table = taps[...].astype(F32)
    lane = lax.broadcasted_iota(jnp.int32, (set_count, time), 1)
    base = jnp.zeros((set_count, time), F32)
    for tap in range(TAPS):
        base = jnp.where((lane + (tap + delay)) % time == 0, table[:, tap : tap + 1], base)
    row_at = lax.broadcasted_iota(jnp.int32, (time, time), 0)
    col_at = lax.broadcasted_iota(jnp.int32, (time, time), 1)
    for index in range(set_count):
        spread = jnp.broadcast_to(base[index : index + 1], (time, time))
        turned = pltpu.roll(spread, 0, 1, stride=1, stride_axis=0)
        band[index] = jnp.where(col_at <= row_at, turned, 0.0).astype(BF16)
        turned = pltpu.roll(spread[:RIM], RIM, 1, stride=1, stride_axis=0)
        band_rim[index] = turned[:, :RIM].astype(BF16)

    pick_row = lax.broadcasted_iota(jnp.int32, (RIM, time), 0)
    pick_col = lax.broadcasted_iota(jnp.int32, (RIM, time), 1)
    pick = jnp.where(pick_col == pick_row + (time - RIM), 1.0, 0.0).astype(BF16)

    def rim_copy(slot, part):
        pair = pl.ds(part * half, half)
        return pltpu.make_async_remote_copy(
            src_ref=rim_out.at[slot, pair],
            dst_ref=rim_in.at[slot, pair],
            send_sem=rim_send.at[slot, part],
            recv_sem=rim_recv.at[slot, part],
            device_id={"tm": lax.rem(block + 1, blocks)},
            device_id_type=MESH,
        )

    def send_rim(slot, part):
        @pl.when(block < blocks - 1)
        def _():
            for ch in range(part * half, (part + 1) * half):
                rim_out[slot, ch] = dot_nt(pick, vbuf[slot, ch]).astype(BF16)
            rim_copy(slot, part).start()

    def wait_rim(slot, part):
        @pl.when(block > 0)
        def _():
            rim_copy(slot, part).wait_recv()

    @pl.when(block == 0)
    def _():
        rim_in[...] = jnp.zeros_like(rim_in)

    def steering(slot, ch):
        real_w = wbuf[slot, ch, :antennas]
        imag_w = wbuf[slot, ch, antennas:]
        upper = jnp.concatenate([real_w, imag_w], axis=1)
        lower = jnp.concatenate([-imag_w, real_w], axis=1)
        return jnp.concatenate([upper, lower], axis=0)

    def filtered(slot, ch):
        chosen = sets[0, block_of(slot) * per + ch]
        return chosen, dot_nt(band[chosen], vbuf[slot, ch])

    def with_rim(slot, ch, chosen, early):
        return early + jnp.dot(band_rim[chosen], rim_in[slot, ch], preferred_element_type=F32)

    def beams(slot, ch):
        chosen, full = filtered(slot, ch)
        early = with_rim(slot, ch, chosen, full[:RIM])
        delayed = jnp.concatenate([early, full[RIM:]], axis=0).astype(BF16)
        return jnp.dot(delayed, steering(slot, ch), preferred_element_type=F32)

    def ring_copy(way, hops, ch, part=None):
        span = pl.ds(0, time) if part is None else part
        return pltpu.make_async_remote_copy(
            src_ref=send.at[way, hops, ch, span],
            dst_ref=recv.at[way, hops, ch, span],
            send_sem=ring_send.at[way, hops, ch],
            recv_sem=ring_recv.at[way, hops, ch],
            device_id={"station": sides[way]},
            device_id_type=MESH,
        )

    def starts(way, hops, ch):
        return reach(way, target_of(way, hops), ch) == hops

    firsts = []
    for back in (0, 1):
        for q in range(half):
            firsts.append((RIGHT, middle - back, back * half + q))
            firsts.append((LEFT, middle - back, (1 - back) * half + q))
    early_span, late_span = pl.ds(0, RIM), pl.ds(RIM, time - RIM)

    def enter_left():
        pl.semaphore_wait(behind_in, 1)

    def late_part(index):
        way, hops, ch = firsts[index]
        slot = slot_of(way, hops)
        chosen, full = filtered(slot, ch)
        top[index] = full[:RIM]
        late = jnp.dot(full[RIM:].astype(BF16), steering(slot, ch), preferred_element_type=F32)
        send[way, hops, ch, RIM:] = late.astype(BF16)

    def early_part(index):
        way, hops, ch = firsts[index]
        slot = slot_of(way, hops)
        chosen = sets[0, block_of(slot) * per + ch]
        early = with_rim(slot, ch, chosen, top[index]).astype(BF16)
        early = jnp.dot(early, steering(slot, ch), preferred_element_type=F32)
        send[way, hops, ch, :RIM] = early.astype(BF16)

    def leave(index, span):
        way, hops, ch = firsts[index]

        @pl.when(starts(way, hops, ch))
        def _():
            ring_copy(way, hops, ch, span).start()

    load(0, 0).wait()
    load(0, 1).wait()
    for index in range(2 * half):
        late_part(index)
    pl.semaphore_wait(barrier, 1 + jnp.where(block < blocks - 1, 1, 0))
    pl.semaphore_signal(behind_in, inc=1, device_id={"station": sides[RIGHT]}, device_id_type=MESH)

    if CUT:

        @pl.when(me > 0)
        def _():
            enter_left()
    else:
        enter_left()

    for index in range(2 * half):
        leave(index, late_span)
    for part in (0, 1):
        send_rim(0, part)
    for slot in (1, 2):
        load(slot, 0).wait()
        send_rim(slot, 2 - slot)
    for slot in (1, 2):
        load(slot, 1).wait()
    for index in range(2 * half, 4 * half):
        late_part(index)
        leave(index, late_span)
    for slot in range(3, ring):
        start_loads(slot)
    for slot in (1, 2):
        send_rim(slot, slot - 1)
    for part in (0, 1):
        wait_rim(0, part)
    for index in range(2 * half):
        early_part(index)
        leave(index, early_span)
    for slot in (1, 2):
        wait_rim(slot, 2 - slot)
    for index in range(2 * half, 4 * half):
        early_part(index)
        leave(index, early_span)

    def prepare(slot):
        load(slot, 0).wait()
        for part in (0, 1):
            send_rim(slot, part)

    def fill(slots):
        for slot in slots:
            load(slot, 1).wait()
            for part in (0, 1):
                wait_rim(slot, part)

    prepare(3)
    prepare(4)
    for slot in (1, 2):
        wait_rim(slot, slot - 1)
    for ch in range(per):
        for slot in (0, 1, 2):
            own[slot, ch] = beams(slot, ch)
    prepare(5)
    prepare(6)

    lags = [0, 0]
    if CUT:
        lags[RIGHT] = jnp.where(jnp.logical_and(me >= 1, me <= CUT), 1, 0)
        lags[LEFT] = jnp.clip((middle - (ring - 1 - me)) // 2, 0, 3)
    order = ([(q + half) % per for q in range(per)], list(range(per)))

    def pass_on(way, hops, ch):
        slot = slot_of(way, hops)
        length = reach(way, target_of(way, hops), ch)
        begun = hops == (middle if (ch < half) == (way == RIGHT) else middle - 1)
        within = jnp.logical_and(hops >= 1, hops <= furthest)

        if CUT:

            @pl.when(jnp.logical_and(within, jnp.logical_and(length == hops, jnp.logical_not(begun))))
            def _():
                send[way, hops, ch] = own[slot, ch].astype(BF16)
                ring_copy(way, hops, ch).start()

        @pl.when(jnp.logical_and(within, length > hops))
        def _():
            ring_copy(way, hops + 1, ch).wait_recv()
            total = own[slot, ch] + recv[way, hops + 1, ch].astype(F32)
            send[way, hops, ch] = total.astype(BF16)
            ring_copy(way, hops, ch).start()

    count = furthest + (3 if CUT else 0)

    @pl.loop(0, count)
    def _(step):
        hops = [furthest - step + lags[way] for way in (RIGHT, LEFT)]
        coming = middle - 2 - step
        slots = [slot_of(way, jnp.maximum(coming, 1)) for way in (RIGHT, LEFT)]

        if CUT:
            @pl.when(jnp.logical_and(me == 0, step == CUT + 1))
            def _():
                enter_left()

        for q in range(per):
            pass_on(LEFT, hops[LEFT], order[LEFT][q])
            pass_on(RIGHT, hops[RIGHT], order[RIGHT][q])

            @pl.when(coming >= 1)
            def _():
                if q == 0:
                    fill(slots)
                for way in (RIGHT, LEFT):
                    ch = order[way][q]
                    own[slots[way], ch] = beams(slots[way], ch)

            @pl.when(coming == 0)
            def _():
                if q == 0:
                    fill((ring - 1,))
                own[ring - 1, q] = beams(ring - 1, q)

        @pl.when(coming >= 3)
        def _():
            for way in (RIGHT, LEFT):
                prepare(slot_of(way, jnp.maximum(coming - 2, 1)))

        @pl.when(coming == 2)
        def _():
            prepare(ring - 1)

    for q in range(per):
        for way in (RIGHT, LEFT):
            ch = order[way][q]
            ring_copy(way, 1, ch).wait_recv()
            total = own[ring - 1, ch] + recv[way, 1, ch].astype(F32)
            if q < half:
                own[ring - 1, ch] = total
            else:
                out[ch] = total.T.astype(BF16)

    @pl.loop(1, furthest + 1)
    def _(hops):
        for way in (RIGHT, LEFT):
            for ch in range(per):

                @pl.when(reach(way, target_of(way, hops), ch) >= hops)
                def _():
                    ring_copy(way, hops, ch).wait_send()

    @pl.when(block < blocks - 1)
    def _():
        @pl.loop(0, ring)
        def _(slot):
            for part in (0, 1):
                rim_copy(slot, part).wait_send()


def body(ring, blocks, voltages, delays, tap_sets, tap_table, weights):
    _, channels, parts, antennas, time = voltages.shape
    beams = weights.shape[-1]
    per = channels // ring
    rows = parts * antennas
    hops = ring // 2 + max(CUT - 1, 0) + 1
    set_count = tap_table.shape[0]
    out = pl.pallas_call(
        functools.partial(kernel, ring, blocks),
        out_shape=jax.ShapeDtypeStruct((per, 2 * beams, time), BF16),
        in_specs=[
            pl.BlockSpec(memory_space=pltpu.HBM),
            pl.BlockSpec(memory_space=pltpu.HBM),
            pl.BlockSpec(memory_space=pltpu.HBM),
            pl.BlockSpec(memory_space=pltpu.SMEM),
            pl.BlockSpec(memory_space=pltpu.HBM),
        ],
        out_specs=pl.BlockSpec(memory_space=pltpu.VMEM),
        scratch_shapes=[
            pltpu.SMEM(tap_sets.shape, jnp.int32),
            pltpu.VMEM(tap_table.shape, BF16),
            pltpu.VMEM((ring, per, rows, time), BF16),
            pltpu.VMEM((ring, per, rows, beams), BF16),
            pltpu.VMEM((ring, per, RIM, rows), BF16),
            pltpu.VMEM((ring, per, RIM, rows), BF16),
            pltpu.VMEM((set_count, time, time), BF16),
            pltpu.VMEM((set_count, RIM, RIM), BF16),
            pltpu.VMEM((2 * per, RIM, rows), F32),
            pltpu.VMEM((ring, per, time, 2 * beams), F32),
            pltpu.VMEM((2, hops, per, time, 2 * beams), BF16),
            pltpu.VMEM((2, hops, per, time, 2 * beams), BF16),
            pltpu.SemaphoreType.DMA((2,)),
            pltpu.SemaphoreType.DMA((ring, 2)),
            pltpu.SemaphoreType.DMA((ring, 2)),
            pltpu.SemaphoreType.DMA((ring, 2)),
            pltpu.SemaphoreType.REGULAR,
            pltpu.SemaphoreType.DMA((2, hops, per)),
            pltpu.SemaphoreType.DMA((2, hops, per)),
        ],
        compiler_params=pltpu.CompilerParams(
            collective_id=0, has_side_effects=True, vmem_limit_bytes=63 * 1024 * 1024
        ),
    )(
        voltages.reshape(channels, rows, time),
        weights.reshape(channels, rows, beams),
        tap_sets,
        delays,
        tap_table,
    )
    return out.reshape(per, 2, beams, time)


def solution(mesh):
    return jax.shard_map(
        functools.partial(body, mesh.shape["station"], mesh.shape["tm"]),
        mesh=mesh,
        in_specs=(
            P(("group", "station"), "chan", None, None, "tm"),
            P(("group", "station")),
            P(("group", "station"), "chan"),
            P(),
            P(("group", "station"), "chan", None, None, None),
        ),
        out_specs=P(("group", "chan", "station"), None, None, "tm"),
        check_vma=False,
    )
```

time: 79.3 us -> 83.1 us (1.048)
  Pallas kernels: 76.7 us -> 80.5 us
    pallas_call x1, Pallas kernels: 76.7 us -> 80.5 us  [body(): pl.pallas_call(functools.partial(kernel, ring, blocks), out_shape=jax.Sha...]
where the time goes in v4:
time: 83.1 us; the launch traced here: 82.8 us
  Pallas kernels  80.5 us (97%)
  local copies, waits for them, and re-layouts  1.67 us (2%)
    pallas_call x1, Pallas kernels, body(): pl.pallas_call(functools.partial(kernel, ring, blocks), out_shape=jax.Sha...  80.5 us
    unnamed x1, local copies, waits for them, and re-layouts  1.67 us

profile of v4, /device:TPU:44, one launch (start us, length us, event | category | flops | bytes accessed | tf_op | source)
XLA Modules:
  0.0 82.8 jit_solution(13020451662705662404)
XLA Ops:
  0.7 80.5 %shard_map.55 = bf16[4,256,128]{2,1,0:T(8,128)(2,1)} custom-call(bf16[64,192,128]{2,1,0:T(8,128)(2,1)} %bitcast.3, bf16[64,192,128]{2,1,0:T(8,128)(2,1)} %bitcast.4, s32[1,64]{1,0:T(1,128)} %sets_hbm.1, s32[1]{0:T(128)S(6)} %copy.7.delays, bf16[16,16]{1,0:T(8,128)(2,1)} %taps_hbm.1), custom_call_target="tpu_custom_call" | custom-call | tf_op jit(solution)/shard_map/pallas_call | solution.py:392
  81.2 1.7 %copy.8 = bf16[4,2,128,128]{3,2,1,0:T(8,128)(2,1)} copy(bf16[4,2,128,128]{3,2,1,0:T(8,128)(2,1)} %bitcast.5) | data formatting | bytes 524288

commit v5 on v4

--- a/solution.py
+++ b/solution.py
@@ -16,7 +16,6 @@
 
 
 RIGHT, LEFT = 0, 1
-CUT = 2
 
 
 def dot_nt(left, right):
@@ -48,7 +47,6 @@
     load_sem,
     rim_send,
     rim_recv,
-    behind_in,
     ring_send,
     ring_recv,
 ):
@@ -63,30 +61,25 @@
     sides = (lax.rem(me + 1, ring), lax.rem(me + ring - 1, ring))
 
     barrier = pltpu.get_barrier_semaphore()
-    pl.semaphore_signal(barrier, inc=1, device_id={"station": sides[LEFT]}, device_id_type=MESH)
+    for side in sides:
+        pl.semaphore_signal(barrier, inc=1, device_id={"station": side}, device_id_type=MESH)
 
     @pl.when(block > 0)
     def _():
         pl.semaphore_signal(barrier, inc=1, device_id={"tm": block - 1}, device_id_type=MESH)
 
-    def reach(way, target, ch):
+    @pl.when(block < blocks - 1)
+    def _():
+        pl.semaphore_signal(barrier, inc=1, device_id={"tm": block + 1}, device_id_type=MESH)
+
+    def reach(way, ch):
         right = middle - ch // half
-        inner = jnp.logical_and(target >= middle - CUT, target < middle + CUT)
-        right = jnp.where(inner, target, right)
         return right if way == RIGHT else ring - 1 - right
-
-    furthest = middle + max(CUT - 1, 0)
-
-    def target_of(way, hops):
-        return lax.rem(me + ring + (hops if way == RIGHT else -hops), ring)
 
     def slot_of(way, hops):
         nearer = middle - hops
         near = 2 * nearer - 1 if way == RIGHT else 2 * nearer
-        far = -2 * nearer if way == RIGHT else -2 * nearer - 1
-        if isinstance(hops, int):
-            return near if nearer > 0 else max(far, 0)
-        return jnp.where(nearer > 0, near, jnp.maximum(far, 0))
+        return max(near, 0) if isinstance(hops, int) else jnp.maximum(near, 0)
 
     def block_of(slot):
         odd = slot % 2
@@ -190,18 +183,12 @@
             device_id_type=MESH,
         )
 
-    def starts(way, hops, ch):
-        return reach(way, target_of(way, hops), ch) == hops
-
     firsts = []
     for back in (0, 1):
         for q in range(half):
             firsts.append((RIGHT, middle - back, back * half + q))
             firsts.append((LEFT, middle - back, (1 - back) * half + q))
     early_span, late_span = pl.ds(0, RIM), pl.ds(RIM, time - RIM)
-
-    def enter_left():
-        pl.semaphore_wait(behind_in, 1)
 
     def late_part(index):
         way, hops, ch = firsts[index]
@@ -221,26 +208,14 @@
 
     def leave(index, span):
         way, hops, ch = firsts[index]
-
-        @pl.when(starts(way, hops, ch))
-        def _():
-            ring_copy(way, hops, ch, span).start()
+        ring_copy(way, hops, ch, span).start()
 
     load(0, 0).wait()
     load(0, 1).wait()
     for index in range(2 * half):
         late_part(index)
-    pl.semaphore_wait(barrier, 1 + jnp.where(block < blocks - 1, 1, 0))
-    pl.semaphore_signal(behind_in, inc=1, device_id={"station": sides[RIGHT]}, device_id_type=MESH)
-
-    if CUT:
-
-        @pl.when(me > 0)
-        def _():
-            enter_left()
-    else:
-        enter_left()
-
+    greeters = 2 + jnp.where(block > 0, 1, 0) + jnp.where(block < blocks - 1, 1, 0)
+    pl.semaphore_wait(barrier, greeters)
     for index in range(2 * half):
         leave(index, late_span)
     for part in (0, 1):
@@ -283,54 +258,33 @@
     prepare(4)
     for slot in (1, 2):
         wait_rim(slot, slot - 1)
-    for ch in range(per):
-        for slot in (0, 1, 2):
-            own[slot, ch] = beams(slot, ch)
+    for ch in range(half):
+        own[1, ch] = beams(1, ch)
+        own[2, ch + half] = beams(2, ch + half)
     prepare(5)
     prepare(6)
 
-    lags = [0, 0]
-    if CUT:
-        lags[RIGHT] = jnp.where(jnp.logical_and(me >= 1, me <= CUT), 1, 0)
-        lags[LEFT] = jnp.clip((middle - (ring - 1 - me)) // 2, 0, 3)
     order = ([(q + half) % per for q in range(per)], list(range(per)))
 
     def pass_on(way, hops, ch):
         slot = slot_of(way, hops)
-        length = reach(way, target_of(way, hops), ch)
-        begun = hops == (middle if (ch < half) == (way == RIGHT) else middle - 1)
-        within = jnp.logical_and(hops >= 1, hops <= furthest)
-
-        if CUT:
-
-            @pl.when(jnp.logical_and(within, jnp.logical_and(length == hops, jnp.logical_not(begun))))
-            def _():
-                send[way, hops, ch] = own[slot, ch].astype(BF16)
-                ring_copy(way, hops, ch).start()
-
-        @pl.when(jnp.logical_and(within, length > hops))
+
+        @pl.when(reach(way, ch) > hops)
         def _():
             ring_copy(way, hops + 1, ch).wait_recv()
             total = own[slot, ch] + recv[way, hops + 1, ch].astype(F32)
             send[way, hops, ch] = total.astype(BF16)
             ring_copy(way, hops, ch).start()
 
-    count = furthest + (3 if CUT else 0)
-
-    @pl.loop(0, count)
+    @pl.loop(1, middle)
     def _(step):
-        hops = [furthest - step + lags[way] for way in (RIGHT, LEFT)]
-        coming = middle - 2 - step
+        hops = middle - step
+        coming = hops - 1
         slots = [slot_of(way, jnp.maximum(coming, 1)) for way in (RIGHT, LEFT)]
 
-        if CUT:
-            @pl.when(jnp.logical_and(me == 0, step == CUT + 1))
-            def _():
-                enter_left()
-
         for q in range(per):
-            pass_on(LEFT, hops[LEFT], order[LEFT][q])
-            pass_on(RIGHT, hops[RIGHT], order[RIGHT][q])
+            pass_on(LEFT, hops, order[LEFT][q])
+            pass_on(RIGHT, hops, order[RIGHT][q])
 
             @pl.when(coming >= 1)
             def _():
@@ -365,12 +319,12 @@
             else:
                 out[ch] = total.T.astype(BF16)
 
-    @pl.loop(1, furthest + 1)
+    @pl.loop(1, middle + 1)
     def _(hops):
         for way in (RIGHT, LEFT):
             for ch in range(per):
 
-                @pl.when(reach(way, target_of(way, hops), ch) >= hops)
+                @pl.when(reach(way, ch) >= hops)
                 def _():
                     ring_copy(way, hops, ch).wait_send()
 
@@ -387,7 +341,7 @@
     beams = weights.shape[-1]
     per = channels // ring
     rows = parts * antennas
-    hops = ring // 2 + max(CUT - 1, 0) + 1
+    hops = ring // 2 + 1
     set_count = tap_table.shape[0]
     out = pl.pallas_call(
         functools.partial(kernel, ring, blocks),
@@ -417,7 +371,6 @@
             pltpu.SemaphoreType.DMA((ring, 2)),
             pltpu.SemaphoreType.DMA((ring, 2)),
             pltpu.SemaphoreType.DMA((ring, 2)),
-            pltpu.SemaphoreType.REGULAR,
             pltpu.SemaphoreType.DMA((2, hops, per)),
             pltpu.SemaphoreType.DMA((2, hops, per)),
         ],

time: 83.1 us -> 77.3 us (0.930)
  Pallas kernels: 80.5 us -> 74.4 us
    pallas_call x1, Pallas kernels: 80.5 us -> 74.4 us  [body(): pl.pallas_call(functools.partial(kernel, ring, blocks), out_shape=jax.Sha...]
where the time goes in v5:
time: 77.3 us; the launch traced here: 76.8 us
  Pallas kernels  74.4 us (96%)
  local copies, waits for them, and re-layouts  1.67 us (2%)
    pallas_call x1, Pallas kernels, body(): pl.pallas_call(functools.partial(kernel, ring, blocks), out_shape=jax.Sha...  74.4 us
    unnamed x1, local copies, waits for them, and re-layouts  1.67 us

profile of v5, /device:TPU:44, one launch (start us, length us, event | category | flops | bytes accessed | tf_op | source)
XLA Modules:
  0.0 76.8 jit_solution(8920290866741232884)
XLA Ops:
  0.7 74.4 %shard_map.55 = bf16[4,256,128]{2,1,0:T(8,128)(2,1)} custom-call(bf16[64,192,128]{2,1,0:T(8,128)(2,1)} %bitcast.3, bf16[64,192,128]{2,1,0:T(8,128)(2,1)} %bitcast.4, s32[1,64]{1,0:T(1,128)} %sets_hbm.1, s32[1]{0:T(128)S(6)} %copy.7.delays, bf16[16,16]{1,0:T(8,128)(2,1)} %taps_hbm.1), custom_call_target="tpu_custom_call" | custom-call | tf_op jit(solution)/shard_map/pallas_call | solution.py:346
  75.1 1.7 %copy.8 = bf16[4,2,128,128]{3,2,1,0:T(8,128)(2,1)} copy(bf16[4,2,128,128]{3,2,1,0:T(8,128)(2,1)} %bitcast.5) | data formatting | bytes 524288

commit v6 on v5

--- a/solution.py
+++ b/solution.py
@@ -15,7 +15,8 @@
 BF16 = jnp.bfloat16
 
 
-RIGHT, LEFT = 0, 1
+OURS, THEIRS = 0, 1
+CUT = 2
 
 
 def dot_nt(left, right):
@@ -41,50 +42,104 @@
     band_rim,
     top,
     own,
+    give,
+    lent,
     send,
+    start,
     recv,
+    last,
     small_sem,
     load_sem,
     rim_send,
     rim_recv,
     ring_send,
+    start_send,
     ring_recv,
+    last_recv,
+    give_send,
+    give_recv,
+    wrap_in,
 ):
     me = lax.axis_index("station")
     block = lax.axis_index("tm")
+    core = lax.axis_index("chan")
+    partner = 1 - core
     per = vbuf.shape[1]
     time = vbuf.shape[3]
     rows = vbuf.shape[2]
     antennas = rows // 2
     set_count = taps.shape[0]
     middle, half = ring // 2, per // 2
-    sides = (lax.rem(me + 1, ring), lax.rem(me + ring - 1, ring))
+    furthest = middle + CUT - 1
+
+    sign = 1 - 2 * core
+    ahead = lax.rem(me + ring + sign, ring)
+    behind = lax.rem(me + ring - sign, ring)
+    right, left = lax.rem(me + 1, ring), lax.rem(me + ring - 1, ring)
 
     barrier = pltpu.get_barrier_semaphore()
-    for side in sides:
-        pl.semaphore_signal(barrier, inc=1, device_id={"station": side}, device_id_type=MESH)
+    first_left = jnp.logical_and(me == 0, core == 1)
+    last_left = jnp.logical_and(me == ring - 1, core == 1)
+    at_wrap = jnp.logical_or(last_left, jnp.logical_and(me == 0, core == 0))
+
+    def greet(**where):
+        pl.semaphore_signal(barrier, inc=1, device_id=where, device_id_type=MESH)
+
+    greet(station=left, chan=0)
+    greet(chan=partner)
+
+    @pl.when(me < ring - 1)
+    def _():
+        greet(station=right, chan=1)
+
+    @pl.when(jnp.logical_not(at_wrap))
+    def _():
+        greet(station=behind, chan=partner)
+
+    @pl.when(first_left)
+    def _():
+        greet(station=left, chan=1)
 
     @pl.when(block > 0)
     def _():
-        pl.semaphore_signal(barrier, inc=1, device_id={"tm": block - 1}, device_id_type=MESH)
-
-    @pl.when(block < blocks - 1)
-    def _():
-        pl.semaphore_signal(barrier, inc=1, device_id={"tm": block + 1}, device_id_type=MESH)
-
-    def reach(way, ch):
-        right = middle - ch // half
-        return right if way == RIGHT else ring - 1 - right
+        greet(tm=block - 1)
+
+    def one(flag):
+        return jnp.where(flag, 1, 0)
+
+    greeters = (
+        3 - 2 * one(first_left) + one(jnp.logical_not(at_wrap)) + one(last_left) + one(block < blocks - 1)
+    )
+
+    def reach(way, target, q):
+        inner = jnp.logical_and(target >= middle - CUT, target < middle + CUT)
+        turned = jnp.where(core == way, target, ring - 1 - target)
+        return jnp.where(inner, turned, middle - q // half)
+
+    def target_of(way, hops):
+        return lax.rem(me + ring + (sign if way == OURS else -sign) * hops, ring)
+
+    def length(way, hops, q):
+        return reach(way, target_of(way, hops), q)
+
+    def channel(way, q):
+        return lax.rem(q + (core if way == OURS else partner) * half, per)
+
+    def is_first(hops, q):
+        return hops == (middle if q < half else middle - 1)
 
     def slot_of(way, hops):
         nearer = middle - hops
-        near = 2 * nearer - 1 if way == RIGHT else 2 * nearer
-        return max(near, 0) if isinstance(hops, int) else jnp.maximum(near, 0)
+        near = 2 * nearer - 1 if way == OURS else 2 * nearer
+        far = -2 * nearer if way == OURS else -2 * nearer - 1
+        if isinstance(hops, int):
+            return near if nearer > 0 else max(far, 0)
+        return jnp.where(nearer > 0, near, jnp.maximum(far, 0))
 
     def block_of(slot):
-        odd = slot % 2
-        distance = jnp.where(odd == 1, ring - (slot + 1) // 2, slot // 2)
-        return lax.rem(me + middle + distance, ring)
+        nearer = middle - (slot + 1) // 2
+        distance = jnp.where(slot % 2 == 1, sign, -sign) * nearer
+        return lax.rem(me + ring + distance, ring)
 
     def load(slot, which):
         source, target = ((volt, vbuf), (steer, wbuf))[which]
@@ -139,7 +194,8 @@
     def send_rim(slot, part):
         @pl.when(block < blocks - 1)
         def _():
-            for ch in range(part * half, (part + 1) * half):
+            for q in range(half):
+                ch = part * half + q
                 rim_out[slot, ch] = dot_nt(pick, vbuf[slot, ch]).astype(BF16)
             rim_copy(slot, part).start()
 
@@ -172,57 +228,103 @@
         delayed = jnp.concatenate([early, full[RIM:]], axis=0).astype(BF16)
         return jnp.dot(delayed, steering(slot, ch), preferred_element_type=F32)
 
-    def ring_copy(way, hops, ch, part=None):
+    def pass_copy(hops, rel, q, part=None):
         span = pl.ds(0, time) if part is None else part
         return pltpu.make_async_remote_copy(
-            src_ref=send.at[way, hops, ch, span],
-            dst_ref=recv.at[way, hops, ch, span],
-            send_sem=ring_send.at[way, hops, ch],
-            recv_sem=ring_recv.at[way, hops, ch],
-            device_id={"station": sides[way]},
+            src_ref=send.at[hops, rel, q, span],
+            dst_ref=recv.at[hops, rel, q, span],
+            send_sem=ring_send.at[hops, rel, q],
+            recv_sem=ring_recv.at[hops, rel, q],
+            device_id={"station": ahead, "chan": core},
+            device_id_type=MESH,
+        )
+
+    def last_copy(way, rel, q):
+        return pltpu.make_async_remote_copy(
+            src_ref=send.at[1, rel, q],
+            dst_ref=last.at[way, q],
+            send_sem=ring_send.at[1, rel, q],
+            recv_sem=last_recv.at[way, q],
+            device_id={"station": ahead, "chan": partner if rel else core},
+            device_id_type=MESH,
+        )
+
+    def start_copy(hops, q, part=None):
+        span = pl.ds(0, time) if part is None else part
+        return pltpu.make_async_remote_copy(
+            src_ref=start.at[hops, q, span],
+            dst_ref=recv.at[hops, 1, q, span],
+            send_sem=start_send.at[hops, q],
+            recv_sem=ring_recv.at[hops, 1, q],
+            device_id={"station": behind, "chan": partner},
+            device_id_type=MESH,
+        )
+
+    def give_copy(hops, q):
+        return pltpu.make_async_remote_copy(
+            src_ref=give.at[hops, q],
+            dst_ref=lent.at[hops, q],
+            send_sem=give_send.at[hops, q],
+            recv_sem=give_recv.at[hops, q],
+            device_id={"chan": partner},
             device_id_type=MESH,
         )
 
     firsts = []
     for back in (0, 1):
         for q in range(half):
-            firsts.append((RIGHT, middle - back, back * half + q))
-            firsts.append((LEFT, middle - back, (1 - back) * half + q))
+            for way in (OURS, THEIRS):
+                firsts.append((way, middle - back, back * half + q))
     early_span, late_span = pl.ds(0, RIM), pl.ds(RIM, time - RIM)
 
+    def put(index, at, value):
+        way, hops, q = firsts[index]
+        if way == OURS:
+            send[hops, 0, q, at] = value.astype(BF16)
+        else:
+            start[hops, q, at] = value.astype(BF16)
+
     def late_part(index):
-        way, hops, ch = firsts[index]
-        slot = slot_of(way, hops)
+        way, hops, q = firsts[index]
+        slot, ch = slot_of(way, hops), channel(way, q)
         chosen, full = filtered(slot, ch)
         top[index] = full[:RIM]
-        late = jnp.dot(full[RIM:].astype(BF16), steering(slot, ch), preferred_element_type=F32)
-        send[way, hops, ch, RIM:] = late.astype(BF16)
+        put(index, late_span, jnp.dot(full[RIM:].astype(BF16), steering(slot, ch), preferred_element_type=F32))
 
     def early_part(index):
-        way, hops, ch = firsts[index]
-        slot = slot_of(way, hops)
+        way, hops, q = firsts[index]
+        slot, ch = slot_of(way, hops), channel(way, q)
         chosen = sets[0, block_of(slot) * per + ch]
         early = with_rim(slot, ch, chosen, top[index]).astype(BF16)
-        early = jnp.dot(early, steering(slot, ch), preferred_element_type=F32)
-        send[way, hops, ch, :RIM] = early.astype(BF16)
+        put(index, early_span, jnp.dot(early, steering(slot, ch), preferred_element_type=F32))
 
     def leave(index, span):
-        way, hops, ch = firsts[index]
-        ring_copy(way, hops, ch, span).start()
+        way, hops, q = firsts[index]
+
+        @pl.when(length(way, hops, q) == hops)
+        def _():
+            if way == OURS:
+                pass_copy(hops, 0, q, span).start()
+            else:
+                start_copy(hops, q, span).start()
 
     load(0, 0).wait()
     load(0, 1).wait()
     for index in range(2 * half):
         late_part(index)
-    greeters = 2 + jnp.where(block > 0, 1, 0) + jnp.where(block < blocks - 1, 1, 0)
     pl.semaphore_wait(barrier, greeters)
+
+    @pl.when(me == ring - 1)
+    def _():
+        pl.semaphore_signal(wrap_in, inc=1, device_id={"station": right, "chan": 1}, device_id_type=MESH)
+
     for index in range(2 * half):
         leave(index, late_span)
     for part in (0, 1):
         send_rim(0, part)
-    for slot in (1, 2):
+    for slot, part in ((1, partner), (2, core)):
         load(slot, 0).wait()
-        send_rim(slot, 2 - slot)
+        send_rim(slot, part)
     for slot in (1, 2):
         load(slot, 1).wait()
     for index in range(2 * half, 4 * half):
@@ -230,15 +332,15 @@
         leave(index, late_span)
     for slot in range(3, ring):
         start_loads(slot)
-    for slot in (1, 2):
-        send_rim(slot, slot - 1)
+    for slot, part in ((1, core), (2, partner)):
+        send_rim(slot, part)
     for part in (0, 1):
         wait_rim(0, part)
     for index in range(2 * half):
         early_part(index)
         leave(index, early_span)
-    for slot in (1, 2):
-        wait_rim(slot, 2 - slot)
+    for slot, part in ((1, partner), (2, core)):
+        wait_rim(slot, part)
     for index in range(2 * half, 4 * half):
         early_part(index)
         leave(index, early_span)
@@ -254,79 +356,134 @@
             for part in (0, 1):
                 wait_rim(slot, part)
 
+    def term(hops, q):
+        reached = length(OURS, hops, q)
+        needed = reached > hops
+        if not isinstance(hops, int) or hops >= middle - 1:
+            begins = jnp.logical_and(reached == hops, jnp.logical_not(is_first(hops, q)))
+            needed = jnp.logical_or(needed, begins)
+
+        @pl.when(needed)
+        def _():
+            own[hops, q] = beams(slot_of(OURS, hops), channel(OURS, q))
+
+        reached = length(THEIRS, hops, q)
+
+        @pl.when(reached > hops)
+        def _():
+            give[hops, q] = beams(slot_of(THEIRS, hops), channel(THEIRS, q))
+            give_copy(hops, q).start()
+
+        @pl.when(jnp.logical_and(reached == hops, jnp.logical_not(is_first(hops, q))))
+        def _():
+            start[hops, q] = beams(slot_of(THEIRS, hops), channel(THEIRS, q)).astype(BF16)
+            start_copy(hops, q).start()
+
+    order = [(q + half) % per for q in range(per)]
     prepare(3)
     prepare(4)
-    for slot in (1, 2):
-        wait_rim(slot, slot - 1)
-    for ch in range(half):
-        own[1, ch] = beams(1, ch)
-        own[2, ch + half] = beams(2, ch + half)
+    for slot, part in ((1, core), (2, partner)):
+        wait_rim(slot, part)
+
+    @pl.loop(0, CUT + 1)
+    def _(step):
+        for q in order:
+            term(furthest - step, q)
+
     prepare(5)
     prepare(6)
 
-    order = ([(q + half) % per for q in range(per)], list(range(per)))
-
-    def pass_on(way, hops, ch):
-        slot = slot_of(way, hops)
-
-        @pl.when(reach(way, ch) > hops)
-        def _():
-            ring_copy(way, hops + 1, ch).wait_recv()
-            total = own[slot, ch] + recv[way, hops + 1, ch].astype(F32)
-            send[way, hops, ch] = total.astype(BF16)
-            ring_copy(way, hops, ch).start()
-
-    @pl.loop(1, middle)
+    def running(hops, rel, q):
+        pass_copy(hops + 1, rel, q).wait_recv()
+        if rel:
+            give_copy(hops, q).wait_recv()
+            term_here = lent[hops, q]
+        else:
+            term_here = own[hops, q]
+        send[hops, rel, q] = (term_here + recv[hops + 1, rel, q].astype(F32)).astype(BF16)
+
+    def pass_on(hops, q):
+        reached = length(OURS, hops, q)
+
+        @pl.when(jnp.logical_and(reached == hops, jnp.logical_not(is_first(hops, q))))
+        def _():
+            send[hops, 0, q] = own[hops, q].astype(BF16)
+            pass_copy(hops, 0, q).start()
+
+        @pl.when(reached > hops)
+        def _():
+            for rel in (0, 1):
+                running(hops, rel, q)
+                pass_copy(hops, rel, q).start()
+
+    @pl.loop(0, furthest - 1)
     def _(step):
-        hops = middle - step
-        coming = hops - 1
-        slots = [slot_of(way, jnp.maximum(coming, 1)) for way in (RIGHT, LEFT)]
-
-        for q in range(per):
-            pass_on(LEFT, hops, order[LEFT][q])
-            pass_on(RIGHT, hops, order[RIGHT][q])
-
-            @pl.when(coming >= 1)
+        hops = furthest - step
+        coming = jnp.maximum(hops - 1, 1)
+        more = hops < middle
+
+        @pl.when(jnp.logical_and(first_left, hops == middle - CUT))
+        def _():
+            pl.semaphore_wait(wrap_in, 2)
+
+        for index, q in enumerate(order):
+            pass_on(hops, q)
+
+            @pl.when(more)
             def _():
-                if q == 0:
-                    fill(slots)
-                for way in (RIGHT, LEFT):
-                    ch = order[way][q]
-                    own[slots[way], ch] = beams(slots[way], ch)
-
-            @pl.when(coming == 0)
-            def _():
-                if q == 0:
-                    fill((ring - 1,))
-                own[ring - 1, q] = beams(ring - 1, q)
-
-        @pl.when(coming >= 3)
-        def _():
-            for way in (RIGHT, LEFT):
-                prepare(slot_of(way, jnp.maximum(coming - 2, 1)))
-
-        @pl.when(coming == 2)
+                if index == 0:
+                    fill([slot_of(way, coming) for way in (OURS, THEIRS)])
+                term(coming, q)
+
+        @pl.when(jnp.logical_and(more, hops >= 4))
+        def _():
+            for way in (OURS, THEIRS):
+                prepare(slot_of(way, jnp.maximum(hops - 3, 1)))
+
+        @pl.when(hops == 3)
         def _():
             prepare(ring - 1)
 
-    for q in range(per):
-        for way in (RIGHT, LEFT):
-            ch = order[way][q]
-            ring_copy(way, 1, ch).wait_recv()
-            total = own[ring - 1, ch] + recv[way, 1, ch].astype(F32)
-            if q < half:
-                own[ring - 1, ch] = total
+    for index, q in enumerate(order):
+        for rel in (0, 1):
+            running(1, rel, q)
+            last_copy(core, rel, q).start()
+        if index == 0:
+            fill((ring - 1,))
+        own[0, q] = beams(ring - 1, q)
+
+    for index, q in enumerate(order):
+        for way in (0, 1):
+            ch = (q + way * half) % per
+            last_copy(way, 0, q).wait_recv()
+            total = own[0, ch] + last[way, q].astype(F32)
+            if index < half:
+                own[0, ch] = total
             else:
                 out[ch] = total.T.astype(BF16)
 
-    @pl.loop(1, middle + 1)
+    @pl.loop(1, furthest + 1)
     def _(hops):
-        for way in (RIGHT, LEFT):
-            for ch in range(per):
-
-                @pl.when(reach(way, ch) >= hops)
-                def _():
-                    ring_copy(way, hops, ch).wait_send()
+        for q in range(per):
+            reached = length(OURS, hops, q)
+
+            @pl.when(reached >= hops)
+            def _():
+                pass_copy(hops, 0, q).wait_send()
+
+            @pl.when(reached > hops)
+            def _():
+                pass_copy(hops, 1, q).wait_send()
+
+            reached = length(THEIRS, hops, q)
+
+            @pl.when(reached == hops)
+            def _():
+                start_copy(hops, q).wait_send()
+
+            @pl.when(reached > hops)
+            def _():
+                give_copy(hops, q).wait_send()
 
     @pl.when(block < blocks - 1)
     def _():
@@ -341,7 +498,7 @@
     beams = weights.shape[-1]
     per = channels // ring
     rows = parts * antennas
-    hops = ring // 2 + 1
+    hops = ring // 2 + CUT
     set_count = tap_table.shape[0]
     out = pl.pallas_call(
         functools.partial(kernel, ring, blocks),
@@ -364,15 +521,24 @@
             pltpu.VMEM((set_count, time, time), BF16),
             pltpu.VMEM((set_count, RIM, RIM), BF16),
             pltpu.VMEM((2 * per, RIM, rows), F32),
-            pltpu.VMEM((ring, per, time, 2 * beams), F32),
-            pltpu.VMEM((2, hops, per, time, 2 * beams), BF16),
-            pltpu.VMEM((2, hops, per, time, 2 * beams), BF16),
+            pltpu.VMEM((hops, per, time, 2 * beams), F32),
+            pltpu.VMEM((hops, per, time, 2 * beams), F32),
+            pltpu.VMEM((hops, per, time, 2 * beams), F32),
+            pltpu.VMEM((hops, 2, per, time, 2 * beams), BF16),
+            pltpu.VMEM((hops, per, time, 2 * beams), BF16),
+            pltpu.VMEM((hops, 2, per, time, 2 * beams), BF16),
+            pltpu.VMEM((2, per, time, 2 * beams), BF16),
             pltpu.SemaphoreType.DMA((2,)),
             pltpu.SemaphoreType.DMA((ring, 2)),
             pltpu.SemaphoreType.DMA((ring, 2)),
             pltpu.SemaphoreType.DMA((ring, 2)),
-            pltpu.SemaphoreType.DMA((2, hops, per)),
-            pltpu.SemaphoreType.DMA((2, hops, per)),
+            pltpu.SemaphoreType.DMA((hops, 2, per)),
+            pltpu.SemaphoreType.DMA((hops, per)),
+            pltpu.SemaphoreType.DMA((hops, 2, per)),
+            pltpu.SemaphoreType.DMA((2, per)),
+            pltpu.SemaphoreType.DMA((hops, per)),
+            pltpu.SemaphoreType.DMA((hops, per)),
+            pltpu.SemaphoreType.REGULAR,
         ],
         compiler_params=pltpu.CompilerParams(
             collective_id=0, has_side_effects=True, vmem_limit_bytes=63 * 1024 * 1024

time: 77.3 us -> 86 us (1.11)
  the two profiles are of different devices: /device:TPU:44 before, /device:TPU:162 now
where the time goes in v6:
time: 86 us; the launch traced here: 85.9 us
  Pallas kernels  83.5 us (97%)
  local copies, waits for them, and re-layouts  1.67 us (2%)
    pallas_call x1, Pallas kernels, body(): pl.pallas_call(functools.partial(kernel, ring, blocks), out_shape=jax.Sha...  83.5 us

profile of v6, /device:TPU:162, one launch (start us, length us, event | category | flops | bytes accessed | tf_op | source)
XLA Modules:
  0.0 85.9 jit_solution(14510207003731205250)
XLA Ops:
  0.7 83.5 %shard_map.55 = bf16[4,256,128]{2,1,0:T(8,128)(2,1)} custom-call(bf16[64,192,128]{2,1,0:T(8,128)(2,1)} %bitcast.3, bf16[64,192,128]{2,1,0:T(8,128)(2,1)} %bitcast.4, s32[1,64]{1,0:T(1,128)} %sets_hbm.1, s32[1]{0:T(128)S(6)} %copy.7.delays, bf16[16,16]{1,0:T(8,128)(2,1)} %taps_hbm.1), custom_call_target="tpu_custom_call" | custom-call | tf_op jit(solution)/shard_map/pallas_call | solution.py:503
  84.2 1.7 %copy.8 = bf16[4,2,128,128]{3,2,1,0:T(8,128)(2,1)} copy(bf16[4,2,128,128]{3,2,1,0:T(8,128)(2,1)} %bitcast.5) | data formatting | bytes 524288

commit v7 on v5

--- a/solution.py
+++ b/solution.py
@@ -286,18 +286,18 @@
             pass_on(LEFT, hops, order[LEFT][q])
             pass_on(RIGHT, hops, order[RIGHT][q])
 
-            @pl.when(coming >= 1)
-            def _():
-                if q == 0:
-                    fill(slots)
+        @pl.when(coming >= 1)
+        def _():
+            fill(slots)
+            for q in range(per):
                 for way in (RIGHT, LEFT):
                     ch = order[way][q]
                     own[slots[way], ch] = beams(slots[way], ch)
 
-            @pl.when(coming == 0)
-            def _():
-                if q == 0:
-                    fill((ring - 1,))
+        @pl.when(coming == 0)
+        def _():
+            fill((ring - 1,))
+            for q in range(per):
                 own[ring - 1, q] = beams(ring - 1, q)
 
         @pl.when(coming >= 3)

time: 77.3 us -> 75.8 us (0.981)
  Pallas kernels: 74.4 us -> 73.3 us
    pallas_call x1, Pallas kernels: 74.4 us -> 73.3 us  [body(): pl.pallas_call(functools.partial(kernel, ring, blocks), out_shape=jax.Sha...]
where the time goes in v7:
time: 75.8 us; the launch traced here: 75.6 us
  Pallas kernels  73.3 us (97%)
  local copies, waits for them, and re-layouts  1.67 us (2%)
    pallas_call x1, Pallas kernels, body(): pl.pallas_call(functools.partial(kernel, ring, blocks), out_shape=jax.Sha...  73.3 us
    unnamed x1, local copies, waits for them, and re-layouts  1.67 us

profile of v7, /device:TPU:44, one launch (start us, length us, event | category | flops | bytes accessed | tf_op | source)
XLA Modules:
  0.0 75.6 jit_solution(17603445477839859288)
XLA Ops:
  0.7 73.3 %shard_map.55 = bf16[4,256,128]{2,1,0:T(8,128)(2,1)} custom-call(bf16[64,192,128]{2,1,0:T(8,128)(2,1)} %bitcast.3, bf16[64,192,128]{2,1,0:T(8,128)(2,1)} %bitcast.4, s32[1,64]{1,0:T(1,128)} %sets_hbm.1, s32[1]{0:T(128)S(6)} %copy.7.delays, bf16[16,16]{1,0:T(8,128)(2,1)} %taps_hbm.1), custom_call_target="tpu_custom_call" | custom-call | tf_op jit(solution)/shard_map/pallas_call | solution.py:346
  74.0 1.7 %copy.8 = bf16[4,2,128,128]{3,2,1,0:T(8,128)(2,1)} copy(bf16[4,2,128,128]{3,2,1,0:T(8,128)(2,1)} %bitcast.5) | data formatting | bytes 524288

commit v8 on v7

--- a/solution.py
+++ b/solution.py
@@ -16,6 +16,7 @@
 
 
 RIGHT, LEFT = 0, 1
+PIECES = 2
 
 
 def dot_nt(left, right):
@@ -58,6 +59,7 @@
     antennas = rows // 2
     set_count = taps.shape[0]
     middle, half = ring // 2, per // 2
+    rows_sent = time // PIECES
     sides = (lax.rem(me + 1, ring), lax.rem(me + ring - 1, ring))
 
     barrier = pltpu.get_barrier_semaphore()
@@ -172,13 +174,13 @@
         delayed = jnp.concatenate([early, full[RIM:]], axis=0).astype(BF16)
         return jnp.dot(delayed, steering(slot, ch), preferred_element_type=F32)
 
-    def ring_copy(way, hops, ch, part=None):
-        span = pl.ds(0, time) if part is None else part
+    def ring_copy(way, hops, ch, piece, part=None):
+        span = pl.ds(piece * rows_sent, rows_sent) if part is None else part
         return pltpu.make_async_remote_copy(
             src_ref=send.at[way, hops, ch, span],
             dst_ref=recv.at[way, hops, ch, span],
-            send_sem=ring_send.at[way, hops, ch],
-            recv_sem=ring_recv.at[way, hops, ch],
+            send_sem=ring_send.at[way, hops, ch, piece],
+            recv_sem=ring_recv.at[way, hops, ch, piece],
             device_id={"station": sides[way]},
             device_id_type=MESH,
         )
@@ -188,7 +190,6 @@
         for q in range(half):
             firsts.append((RIGHT, middle - back, back * half + q))
             firsts.append((LEFT, middle - back, (1 - back) * half + q))
-    early_span, late_span = pl.ds(0, RIM), pl.ds(RIM, time - RIM)
 
     def late_part(index):
         way, hops, ch = firsts[index]
@@ -206,18 +207,23 @@
         early = jnp.dot(early, steering(slot, ch), preferred_element_type=F32)
         send[way, hops, ch, :RIM] = early.astype(BF16)
 
-    def leave(index, span):
+    def leave_late(index):
         way, hops, ch = firsts[index]
-        ring_copy(way, hops, ch, span).start()
+        for piece in range(1, PIECES):
+            ring_copy(way, hops, ch, piece).start()
+        ring_copy(way, hops, ch, 0, pl.ds(RIM, rows_sent - RIM)).start()
+
+    def leave_early(index):
+        way, hops, ch = firsts[index]
+        ring_copy(way, hops, ch, 0, pl.ds(0, RIM)).start()
 
     load(0, 0).wait()
     load(0, 1).wait()
-    for index in range(2 * half):
-        late_part(index)
     greeters = 2 + jnp.where(block > 0, 1, 0) + jnp.where(block < blocks - 1, 1, 0)
     pl.semaphore_wait(barrier, greeters)
     for index in range(2 * half):
-        leave(index, late_span)
+        late_part(index)
+        leave_late(index)
     for part in (0, 1):
         send_rim(0, part)
     for slot in (1, 2):
@@ -227,7 +233,7 @@
         load(slot, 1).wait()
     for index in range(2 * half, 4 * half):
         late_part(index)
-        leave(index, late_span)
+        leave_late(index)
     for slot in range(3, ring):
         start_loads(slot)
     for slot in (1, 2):
@@ -236,12 +242,12 @@
         wait_rim(0, part)
     for index in range(2 * half):
         early_part(index)
-        leave(index, early_span)
+        leave_early(index)
     for slot in (1, 2):
         wait_rim(slot, 2 - slot)
     for index in range(2 * half, 4 * half):
         early_part(index)
-        leave(index, early_span)
+        leave_early(index)
 
     def prepare(slot):
         load(slot, 0).wait()
@@ -266,15 +272,19 @@
 
     order = ([(q + half) % per for q in range(per)], list(range(per)))
 
+    pieces = list(range(1, PIECES)) + [0]
+
     def pass_on(way, hops, ch):
         slot = slot_of(way, hops)
 
         @pl.when(reach(way, ch) > hops)
         def _():
-            ring_copy(way, hops + 1, ch).wait_recv()
-            total = own[slot, ch] + recv[way, hops + 1, ch].astype(F32)
-            send[way, hops, ch] = total.astype(BF16)
-            ring_copy(way, hops, ch).start()
+            for piece in pieces:
+                at = pl.ds(piece * rows_sent, rows_sent)
+                ring_copy(way, hops + 1, ch, piece).wait_recv()
+                total = own[slot, ch, at] + recv[way, hops + 1, ch, at].astype(F32)
+                send[way, hops, ch, at] = total.astype(BF16)
+                ring_copy(way, hops, ch, piece).start()
 
     @pl.loop(1, middle)
     def _(step):
@@ -312,12 +322,13 @@
     for q in range(per):
         for way in (RIGHT, LEFT):
             ch = order[way][q]
-            ring_copy(way, 1, ch).wait_recv()
-            total = own[ring - 1, ch] + recv[way, 1, ch].astype(F32)
-            if q < half:
-                own[ring - 1, ch] = total
-            else:
-                out[ch] = total.T.astype(BF16)
+            for piece in pieces:
+                at = pl.ds(piece * rows_sent, rows_sent)
+                ring_copy(way, 1, ch, piece).wait_recv()
+                total = own[ring - 1, ch, at] + recv[way, 1, ch, at].astype(F32)
+                own[ring - 1, ch, at] = total
+            if q >= half:
+                out[ch] = own[ring - 1, ch].T.astype(BF16)
 
     @pl.loop(1, middle + 1)
     def _(hops):
@@ -326,7 +337,8 @@
 
                 @pl.when(reach(way, ch) >= hops)
                 def _():
-                    ring_copy(way, hops, ch).wait_send()
+                    for piece in pieces:
+                        ring_copy(way, hops, ch, piece).wait_send()
 
     @pl.when(block < blocks - 1)
     def _():
@@ -371,8 +383,8 @@
             pltpu.SemaphoreType.DMA((ring, 2)),
             pltpu.SemaphoreType.DMA((ring, 2)),
             pltpu.SemaphoreType.DMA((ring, 2)),
-            pltpu.SemaphoreType.DMA((2, hops, per)),
-            pltpu.SemaphoreType.DMA((2, hops, per)),
+            pltpu.SemaphoreType.DMA((2, hops, per, PIECES)),
+            pltpu.SemaphoreType.DMA((2, hops, per, PIECES)),
         ],
         compiler_params=pltpu.CompilerParams(
             collective_id=0, has_side_effects=True, vmem_limit_bytes=63 * 1024 * 1024

time: 75.8 us -> 78.3 us (1.033)
  Pallas kernels: 73.3 us -> 75.8 us
    pallas_call x1, Pallas kernels: 73.3 us -> 75.8 us  [body(): pl.pallas_call(functools.partial(kernel, ring, blocks), out_shape=jax.Sha...]
where the time goes in v8:
time: 78.3 us; the launch traced here: 78.1 us
  Pallas kernels  75.8 us (97%)
  local copies, waits for them, and re-layouts  1.67 us (2%)
    pallas_call x1, Pallas kernels, body(): pl.pallas_call(functools.partial(kernel, ring, blocks), out_shape=jax.Sha...  75.8 us
    unnamed x1, local copies, waits for them, and re-layouts  1.67 us

profile of v8, /device:TPU:44, one launch (start us, length us, event | category | flops | bytes accessed | tf_op | source)
XLA Modules:
  0.0 78.1 jit_solution(17377132871636865653)
XLA Ops:
  0.7 75.8 %shard_map.55 = bf16[4,256,128]{2,1,0:T(8,128)(2,1)} custom-call(bf16[64,192,128]{2,1,0:T(8,128)(2,1)} %bitcast.3, bf16[64,192,128]{2,1,0:T(8,128)(2,1)} %bitcast.4, s32[1,64]{1,0:T(1,128)} %sets_hbm.1, s32[1]{0:T(128)S(6)} %copy.7.delays, bf16[16,16]{1,0:T(8,128)(2,1)} %taps_hbm.1), custom_call_target="tpu_custom_call" | custom-call | tf_op jit(solution)/shard_map/pallas_call | solution.py:358
  76.5 1.7 %copy.8 = bf16[4,2,128,128]{3,2,1,0:T(8,128)(2,1)} copy(bf16[4,2,128,128]{3,2,1,0:T(8,128)(2,1)} %bitcast.5) | data formatting | bytes 524288

commit v9 on v5

--- a/solution.py
+++ b/solution.py
@@ -212,11 +212,10 @@
 
     load(0, 0).wait()
     load(0, 1).wait()
-    for index in range(2 * half):
-        late_part(index)
     greeters = 2 + jnp.where(block > 0, 1, 0) + jnp.where(block < blocks - 1, 1, 0)
     pl.semaphore_wait(barrier, greeters)
     for index in range(2 * half):
+        late_part(index)
         leave(index, late_span)
     for part in (0, 1):
         send_rim(0, part)
@@ -282,17 +281,23 @@
         coming = hops - 1
         slots = [slot_of(way, jnp.maximum(coming, 1)) for way in (RIGHT, LEFT)]
 
+        early = hops == middle - 1
+        rims = [slot_of(way, jnp.maximum(coming - 2, 1)) for way in (RIGHT, LEFT)]
+
+        def terms(q):
+            for way in (RIGHT, LEFT):
+                ch = order[way][q]
+                own[slots[way], ch] = beams(slots[way], ch)
+
         for q in range(per):
             pass_on(LEFT, hops, order[LEFT][q])
             pass_on(RIGHT, hops, order[RIGHT][q])
 
-            @pl.when(coming >= 1)
+            @pl.when(jnp.logical_and(coming >= 1, jnp.logical_not(early)))
             def _():
                 if q == 0:
                     fill(slots)
-                for way in (RIGHT, LEFT):
-                    ch = order[way][q]
-                    own[slots[way], ch] = beams(slots[way], ch)
+                terms(q)
 
             @pl.when(coming == 0)
             def _():
@@ -300,10 +305,18 @@
                     fill((ring - 1,))
                 own[ring - 1, q] = beams(ring - 1, q)
 
-        @pl.when(coming >= 3)
+            @pl.when(coming >= 3)
+            def _():
+                slot, part = rims[q // 2], q % 2
+                if part == 0:
+                    load(slot, 0).wait()
+                send_rim(slot, part)
+
+        @pl.when(early)
         def _():
-            for way in (RIGHT, LEFT):
-                prepare(slot_of(way, jnp.maximum(coming - 2, 1)))
+            fill(slots)
+            for q in range(per):
+                terms(q)
 
         @pl.when(coming == 2)
         def _():

time: 77.3 us -> 77.2 us (level)
  no operation moved by 1% of the time
where the time goes in v9:
time: 77.2 us; the launch traced here: 77.1 us
  Pallas kernels  74.7 us (97%)
  local copies, waits for them, and re-layouts  1.67 us (2%)
    pallas_call x1, Pallas kernels, body(): pl.pallas_call(functools.partial(kernel, ring, blocks), out_shape=jax.Sha...  74.7 us
    unnamed x1, local copies, waits for them, and re-layouts  1.67 us

profile of v9, /device:TPU:44, one launch (start us, length us, event | category | flops | bytes accessed | tf_op | source)
XLA Modules:
  0.0 77.1 jit_solution(16438760614612754894)
XLA Ops:
  0.7 74.7 %shard_map.55 = bf16[4,256,128]{2,1,0:T(8,128)(2,1)} custom-call(bf16[64,192,128]{2,1,0:T(8,128)(2,1)} %bitcast.3, bf16[64,192,128]{2,1,0:T(8,128)(2,1)} %bitcast.4, s32[1,64]{1,0:T(1,128)} %sets_hbm.1, s32[1]{0:T(128)S(6)} %copy.7.delays, bf16[16,16]{1,0:T(8,128)(2,1)} %taps_hbm.1), custom_call_target="tpu_custom_call" | custom-call | tf_op jit(solution)/shard_map/pallas_call | solution.py:359
  75.4 1.7 %copy.8 = bf16[4,2,128,128]{3,2,1,0:T(8,128)(2,1)} copy(bf16[4,2,128,128]{3,2,1,0:T(8,128)(2,1)} %bitcast.5) | data formatting | bytes 524288

commit v10 on v7

--- a/solution.py
+++ b/solution.py
@@ -101,10 +101,11 @@
     ]
     for copy in small:
         copy.start()
-    for slot in range(3):
-        start_loads(slot)
+    start_loads(0)
     for copy in small:
         copy.wait()
+    for slot in (1, 2):
+        start_loads(slot)
 
     delay = delays[0]
     table = taps[...].astype(F32)
@@ -211,32 +212,32 @@
         ring_copy(way, hops, ch, span).start()
 
     load(0, 0).wait()
+    greeters = 2 + jnp.where(block > 0, 1, 0) + jnp.where(block < blocks - 1, 1, 0)
+    pl.semaphore_wait(barrier, greeters)
+    for part in (0, 1):
+        send_rim(0, part)
     load(0, 1).wait()
     for index in range(2 * half):
         late_part(index)
-    greeters = 2 + jnp.where(block > 0, 1, 0) + jnp.where(block < blocks - 1, 1, 0)
-    pl.semaphore_wait(barrier, greeters)
-    for index in range(2 * half):
         leave(index, late_span)
-    for part in (0, 1):
-        send_rim(0, part)
     for slot in (1, 2):
         load(slot, 0).wait()
         send_rim(slot, 2 - slot)
+    for slot in range(3, ring):
+        start_loads(slot)
     for slot in (1, 2):
         load(slot, 1).wait()
     for index in range(2 * half, 4 * half):
         late_part(index)
-        leave(index, late_span)
-    for slot in range(3, ring):
-        start_loads(slot)
-    for slot in (1, 2):
-        send_rim(slot, slot - 1)
     for part in (0, 1):
         wait_rim(0, part)
     for index in range(2 * half):
         early_part(index)
         leave(index, early_span)
+    for index in range(2 * half, 4 * half):
+        leave(index, late_span)
+    for slot in (1, 2):
+        send_rim(slot, slot - 1)
     for slot in (1, 2):
         wait_rim(slot, 2 - slot)
     for index in range(2 * half, 4 * half):

time: 75.8 us -> 76.4 us (level)
  no operation moved by 1% of the time
where the time goes in v10:
time: 76.4 us; the launch traced here: 76.3 us
  Pallas kernels  74 us (97%)
  local copies, waits for them, and re-layouts  1.67 us (2%)
    pallas_call x1, Pallas kernels, body(): pl.pallas_call(functools.partial(kernel, ring, blocks), out_shape=jax.Sha...  74 us
    unnamed x1, local copies, waits for them, and re-layouts  1.67 us

profile of v10, /device:TPU:44, one launch (start us, length us, event | category | flops | bytes accessed | tf_op | source)
XLA Modules:
  0.0 76.3 jit_solution(16397022186629782814)
XLA Ops:
  0.7 74.0 %shard_map.55 = bf16[4,256,128]{2,1,0:T(8,128)(2,1)} custom-call(bf16[64,192,128]{2,1,0:T(8,128)(2,1)} %bitcast.3, bf16[64,192,128]{2,1,0:T(8,128)(2,1)} %bitcast.4, s32[1,64]{1,0:T(1,128)} %sets_hbm.1, s32[1]{0:T(128)S(6)} %copy.7.delays, bf16[16,16]{1,0:T(8,128)(2,1)} %taps_hbm.1), custom_call_target="tpu_custom_call" | custom-call | tf_op jit(solution)/shard_map/pallas_call | solution.py:347
  74.6 1.7 %copy.8 = bf16[4,2,128,128]{3,2,1,0:T(8,128)(2,1)} copy(bf16[4,2,128,128]{3,2,1,0:T(8,128)(2,1)} %bitcast.5) | data formatting | bytes 524288

commit v11 on v7

--- a/solution.py
+++ b/solution.py
@@ -375,7 +375,7 @@
             pltpu.SemaphoreType.DMA((2, hops, per)),
         ],
         compiler_params=pltpu.CompilerParams(
-            collective_id=0, has_side_effects=True, vmem_limit_bytes=63 * 1024 * 1024
+            collective_id=0, has_side_effects=True, vmem_limit_bytes=53 * 1024 * 1024
         ),
     )(
         voltages.reshape(channels, rows, time),

time: 75.8 us -> 75.3 us (level)
  Pallas kernels: 73.3 us -> 72.4 us
    pallas_call x1, Pallas kernels: 73.3 us -> 72.4 us  [body(): pl.pallas_call(functools.partial(kernel, ring, blocks), out_shape=jax.Sha...]
    unnamed x1 -> x5, local copies, waits for them, and re-layouts: 1.67 us -> 2.04 us
where the time goes in v11:
time: 75.3 us; the launch traced here: 75.1 us
  Pallas kernels  72.4 us (96%)
  local copies, waits for them, and re-layouts  2.04 us (3%)
    pallas_call x1, Pallas kernels, body(): pl.pallas_call(functools.partial(kernel, ring, blocks), out_shape=jax.Sha...  72.4 us
    unnamed x5, local copies, waits for them, and re-layouts  2.04 us

profile of v11, /device:TPU:44, one launch (start us, length us, event | category | flops | bytes accessed | tf_op | source)
XLA Modules:
  0.0 75.1 jit_solution(1085978104809651478)
XLA Ops:
  0.7 0.0 copy-start
  0.7 0.7 copy-done
  1.3 0.0 copy-start.1
  1.3 0.7 copy-done.1
  2.0 72.4 %shard_map.55 = bf16[4,256,128]{2,1,0:T(8,128)(2,1)S(1)} custom-call(bf16[64,192,128]{2,1,0:T(8,128)(2,1)} %bitcast.4, bf16[64,192,128]{2,1,0:T(8,128)(2,1)} %bitcast.5, s32[1,64]{1,0:T(1,128)S(1)} %copy-done.1, s32[1]{0:T(128)S(6)} %copy.7.delays, bf16[16,16]{1,0:T(8,128)(2,1)S(1)} %copy-done), custom_call_target="tpu_custom_call" | custom-call | tf_op jit(solution)/shard_map/pallas_call | solution.py:346
  74.4 0.7 copy.8
Async XLA Ops:
  0.7 0.7 copy-start
  1.3 0.7 copy-start.1

commit v12 on v11

--- a/solution.py
+++ b/solution.py
@@ -52,6 +52,7 @@
 ):
     me = lax.axis_index("station")
     block = lax.axis_index("tm")
+    core = lax.axis_index("chan")
     per = vbuf.shape[1]
     time = vbuf.shape[3]
     rows = vbuf.shape[2]
@@ -266,10 +267,10 @@
 
     order = ([(q + half) % per for q in range(per)], list(range(per)))
 
-    def pass_on(way, hops, ch):
+    def pass_on(way, hops, ch, now):
         slot = slot_of(way, hops)
 
-        @pl.when(reach(way, ch) > hops)
+        @pl.when(jnp.logical_and(reach(way, ch) > hops, now))
         def _():
             ring_copy(way, hops + 1, ch).wait_recv()
             total = own[slot, ch] + recv[way, hops + 1, ch].astype(F32)
@@ -283,8 +284,9 @@
         slots = [slot_of(way, jnp.maximum(coming, 1)) for way in (RIGHT, LEFT)]
 
         for q in range(per):
-            pass_on(LEFT, hops, order[LEFT][q])
-            pass_on(RIGHT, hops, order[RIGHT][q])
+            pass_on(LEFT, hops, order[LEFT][q], core == 0)
+            pass_on(RIGHT, hops, order[RIGHT][q], True)
+            pass_on(LEFT, hops, order[LEFT][q], core == 1)
 
         @pl.when(coming >= 1)
         def _():

time: 75.3 us -> 75.3 us (level)
  no operation moved by 1% of the time
where the time goes in v12:
time: 75.3 us; the launch traced here: 75.1 us
  Pallas kernels  72.4 us (96%)
  local copies, waits for them, and re-layouts  2.04 us (3%)
    pallas_call x1, Pallas kernels, body(): pl.pallas_call(functools.partial(kernel, ring, blocks), out_shape=jax.Sha...  72.4 us
    unnamed x5, local copies, waits for them, and re-layouts  2.04 us

profile of v12, /device:TPU:44, one launch (start us, length us, event | category | flops | bytes accessed | tf_op | source)
XLA Modules:
  0.0 75.1 jit_solution(12113257123125710217)
XLA Ops:
  0.7 0.0 copy-start
  0.7 0.7 copy-done
  1.3 0.0 copy-start.1
  1.3 0.7 copy-done.1
  2.0 72.4 %shard_map.55 = bf16[4,256,128]{2,1,0:T(8,128)(2,1)S(1)} custom-call(bf16[64,192,128]{2,1,0:T(8,128)(2,1)} %bitcast.4, bf16[64,192,128]{2,1,0:T(8,128)(2,1)} %bitcast.5, s32[1,64]{1,0:T(1,128)S(1)} %copy-done.1, s32[1]{0:T(128)S(6)} %copy.7.delays, bf16[16,16]{1,0:T(8,128)(2,1)S(1)} %copy-done), custom_call_target="tpu_custom_call" | custom-call | tf_op jit(solution)/shard_map/pallas_call | solution.py:348
  74.4 0.7 copy.8
Async XLA Ops:
  0.7 0.7 copy-start
  1.3 0.7 copy-start.1

commit v13 on v11

--- a/solution.py
+++ b/solution.py
@@ -286,6 +286,15 @@
             pass_on(LEFT, hops, order[LEFT][q])
             pass_on(RIGHT, hops, order[RIGHT][q])
 
+        @pl.when(coming >= 3)
+        def _():
+            for way in (RIGHT, LEFT):
+                prepare(slot_of(way, jnp.maximum(coming - 2, 1)))
+
+        @pl.when(coming == 2)
+        def _():
+            prepare(ring - 1)
+
         @pl.when(coming >= 1)
         def _():
             fill(slots)
@@ -299,15 +308,6 @@
             fill((ring - 1,))
             for q in range(per):
                 own[ring - 1, q] = beams(ring - 1, q)
-
-        @pl.when(coming >= 3)
-        def _():
-            for way in (RIGHT, LEFT):
-                prepare(slot_of(way, jnp.maximum(coming - 2, 1)))
-
-        @pl.when(coming == 2)
-        def _():
-            prepare(ring - 1)
 
     for q in range(per):
         for way in (RIGHT, LEFT):

time: 75.3 us -> 75.3 us (level)
  no operation moved by 1% of the time
where the time goes in v13:
time: 75.3 us; the launch traced here: 75.1 us
  Pallas kernels  72.4 us (96%)
  local copies, waits for them, and re-layouts  2.04 us (3%)
    pallas_call x1, Pallas kernels, body(): pl.pallas_call(functools.partial(kernel, ring, blocks), out_shape=jax.Sha...  72.4 us
    unnamed x5, local copies, waits for them, and re-layouts  2.04 us

profile of v13, /device:TPU:44, one launch (start us, length us, event | category | flops | bytes accessed | tf_op | source)
XLA Modules:
  0.0 75.1 jit_solution(1276941092524231146)
XLA Ops:
  0.7 0.0 copy-start
  0.7 0.7 copy-done
  1.3 0.0 copy-start.1
  1.3 0.7 copy-done.1
  2.0 72.4 %shard_map.55 = bf16[4,256,128]{2,1,0:T(8,128)(2,1)S(1)} custom-call(bf16[64,192,128]{2,1,0:T(8,128)(2,1)} %bitcast.4, bf16[64,192,128]{2,1,0:T(8,128)(2,1)} %bitcast.5, s32[1,64]{1,0:T(1,128)S(1)} %copy-done.1, s32[1]{0:T(128)S(6)} %copy.7.delays, bf16[16,16]{1,0:T(8,128)(2,1)S(1)} %copy-done), custom_call_target="tpu_custom_call" | custom-call | tf_op jit(solution)/shard_map/pallas_call | solution.py:346
  74.4 0.7 copy.8
Async XLA Ops:
  0.7 0.7 copy-start
  1.3 0.7 copy-start.1
